TPU v7x, 128 devices: a whole 4x4x4 slice. The times are simulated.
128 devices in a mesh: expert: 16 (over y, z), width: 8 (over x, core).
Axes of the slice: x: 4, y: 4, z: 4, core: 2. Of those that a mesh axis runs over, the one named last changes fastest.
Arguments:
- tokens_in: bfloat16 [6144, 7168], P('expert', 'width'), may hold values from -6 to 6
- out_grad: bfloat16 [6144, 7168], P('expert', 'width'), may hold values from -0.08984375 to 0.08984375
- router_weight: bfloat16 [7168, 256], P('width'), may hold values from -0.0625 to 0.0625
- expert_out: bfloat16 [49152, 7168], P('expert', 'width'), may hold values from -6 to 6
- expert_ids: int32 [6144, 8], P('expert'), may hold values from 0 to 255, as said below
- slot_ids: int32 [6144, 8], P('expert'), may hold values from 0 to 191, as said below
Outputs:
- expert_grad: bfloat16 [49152, 7168], P('expert', 'width')
- router_grad: float32 [7168, 256], P('width', 'expert')
- input_grad: bfloat16 [6144, 7168], P('expert', 'width')
Inputs may be any that keep to these rules, and one draw needn't show every extreme that they name: `expert_ids`: expert e lies on device e // 16 of the expert axis; a token's 8 experts lie on 8 different devices. The tokens of each device choose experts of each device of the expert axis exactly 192 times. slot_ids[t, k] is the row, within the block of 192 rows that token t's device sends to the device of expert expert_ids[t, k], of that pair. The pairs of one block fill all its rows, grouped by expert in rising order and by token in rising order within an expert. The values of expert_ids and slot_ids fit in 8 bits each, and both may be sent packed several to a 32-bit word.
All inputs are finite; a program needn't handle non-finite values.
Results may differ from a plain program's by a relative error of at most 0.015.
Values may be sent and summed in bfloat16 or wider, within the bound.
A program may use at most 128 MiB of HBM per device.

v0:
```python
import jax
import jax.numpy as jnp
from jax import lax
from jax.sharding import PartitionSpec as P

route_scale = 2.5


def copy_for_each(x, axis):
    length = lax.axis_size(axis)
    return lax.all_to_all(jnp.broadcast_to(x[None], (length, *x.shape)), axis, 0, 0, tiled=True)


def over_copies(x, axis):
    return copy_for_each(x, axis).astype(jnp.float32).sum(axis=0)


def sent_together(arrays, axis, dim, along):
    both = jnp.concatenate(arrays, axis=along)
    result, at, gathered = (lax.all_gather(both, axis, axis=dim, tiled=True), 0, [])
    for a in arrays:
        gathered.append(lax.slice_in_dim(result, at, at + a.shape[along], axis=along))
        at += a.shape[along]
    return tuple(gathered)


def over_copies_2(x, axis):
    everything = copy_for_each(x, axis)
    return jnp.sum(everything, axis=0)


def split_up(x, dim, length):
    shape = x.shape
    blocks = x.reshape(*shape[:dim], length, shape[dim] // length, *shape[dim + 1 :])
    return jnp.moveaxis(blocks, dim, 0)


def sum_at_owner(x, axis, dim):
    length = lax.axis_size(axis)
    blocks = lax.all_to_all(split_up(x, dim, length), axis, 0, 0, tiled=True)
    return jnp.sum(blocks.astype(jnp.float32), axis=0)


def gate_parts(logits, expert_ids):
    scores = jax.nn.sigmoid(logits)
    expert_count = logits.shape[1]
    matches = expert_ids[:, :, None] == jnp.arange(expert_count, dtype=jnp.int32)[None, None, :]
    picked = jnp.sum(jnp.where(matches, scores[:, None, :], 0.0), axis=2)
    totals = jnp.sum(picked, axis=1, keepdims=True)
    return (picked, totals)


def logit_gradient(gate_grads, picked, totals, expert_ids, expert_count):
    weighted = jnp.sum(gate_grads * picked, axis=1, keepdims=True) / totals
    score_grads = route_scale / totals * (gate_grads - weighted)
    local_grads = score_grads * picked * (1.0 - picked)
    matches = expert_ids[:, :, None] == jnp.arange(expert_count, dtype=jnp.int32)[None, None, :]
    return jnp.sum(jnp.where(matches, local_grads[:, :, None], 0.0), axis=1).astype(jnp.bfloat16)


def pair_table(dest_dev, dest_slot, dev_count, capacity):
    dev_match = jnp.arange(dev_count, dtype=jnp.int32)[:, None, None] == dest_dev[None, None, :]
    slot_match = jnp.arange(capacity, dtype=jnp.int32)[None, :, None] == dest_slot[None, None, :]
    return jnp.logical_and(dev_match, slot_match)


def spread_values(values, dest_ids, slot_ids, per_device, dev_count, capacity):
    total = jnp.zeros((dev_count, capacity), jnp.float32)
    for pick in range(values.shape[1]):
        table = pair_table(dest_ids[:, pick] // per_device, slot_ids[:, pick], dev_count, capacity)
        total = total + jnp.sum(jnp.where(table, values[:, pick][None, None, :], 0.0), axis=2)
    return total.reshape(-1)


def collect_values(flat_values, dest_ids, slot_ids, per_device, dev_count, capacity):
    grid = flat_values.reshape(dev_count, capacity)
    columns = []
    for pick in range(dest_ids.shape[1]):
        table = pair_table(dest_ids[:, pick] // per_device, slot_ids[:, pick], dev_count, capacity)
        columns.append(jnp.sum(jnp.where(table, grid[:, :, None], 0.0), axis=(0, 1)))
    return jnp.stack(columns, axis=1)


def body(tokens_in, out_grad, router_weight, expert_out, expert_ids, slot_ids):
    dev_count = lax.axis_size("expert")
    own_index = lax.axis_index("expert")
    tok_rows, width_cols = out_grad.shape
    top_count = expert_ids.shape[1]
    expert_count = router_weight.shape[1]
    per_device = expert_count // dev_count
    capacity = tok_rows * top_count // dev_count
    buffer_rows = dev_count * capacity
    width_part = jnp.dot(tokens_in, router_weight, preferred_element_type=jnp.float32)
    logits = over_copies(width_part.astype(jnp.bfloat16), "width").astype(jnp.float32)
    picked, totals = gate_parts(logits, expert_ids)
    gate_weights = (route_scale * picked / totals).astype(jnp.bfloat16)
    gate_f32 = gate_weights.astype(jnp.float32)
    all_grads = lax.all_gather(out_grad, "expert", axis=0, tiled=True)
    all_ids, all_slots = sent_together((expert_ids, slot_ids), "expert", 0, 1)
    mine = all_ids // per_device == own_index
    has_mine = jnp.any(mine, axis=1).reshape(dev_count, tok_rows)
    slot_mine = jnp.sum(jnp.where(mine, all_slots, 0), axis=1).reshape(dev_count, tok_rows)
    slot_match = jnp.arange(capacity, dtype=jnp.int32)[None, :, None] == slot_mine[:, None, :]
    routing = jnp.logical_and(slot_match, has_mine[:, None, :]).astype(jnp.bfloat16)
    grads_grid = all_grads.reshape(dev_count, tok_rows, width_cols)
    routed = jnp.einsum("sct,stw->scw", routing, grads_grid, preferred_element_type=jnp.float32)
    received = routed.astype(jnp.bfloat16).reshape(buffer_rows, width_cols)
    dot_parts = jnp.einsum("rd,rd->r", received, expert_out, preferred_element_type=jnp.float32)
    dot_totals = over_copies_2(dot_parts, "width")
    gate_buffer = spread_values(gate_f32, expert_ids, slot_ids, per_device, dev_count, capacity)
    returned, gate_values = (
        lax.all_to_all(dot_totals, "expert", split_axis=0, concat_axis=0, tiled=True),
        lax.all_to_all(gate_buffer, "expert", split_axis=0, concat_axis=0, tiled=True),
    )
    expert_grad = (gate_values[:, None] * received.astype(jnp.float32)).astype(jnp.bfloat16)
    gate_grads = collect_values(returned, expert_ids, slot_ids, per_device, dev_count, capacity)
    logit_grads = logit_gradient(gate_grads, picked, totals, expert_ids, expert_count)
    router_part = lax.dot_general(
        tokens_in, logit_grads, (((0,), (0,)), ((), ())), preferred_element_type=jnp.float32
    )
    router_grad = sum_at_owner(router_part.astype(jnp.bfloat16), "expert", 1)
    input_grad = lax.dot_general(
        logit_grads, router_weight, (((1,), (1,)), ((), ())), preferred_element_type=jnp.float32
    ).astype(jnp.bfloat16)
    return (expert_grad, router_grad, input_grad)


def solution(mesh):
    return jax.shard_map(
        body,
        mesh=mesh,
        in_specs=(
            P("expert", "width"),
            P("expert", "width"),
            P("width", None),
            P("expert", "width"),
            P("expert", None),
            P("expert", None),
        ),
        out_specs=(P("expert", "width"), P("width", "expert"), P("expert", "width")),
        check_vma=False,
    )
```

profile of v0, /device:TPU:0, one launch (start us, length us, event | category | flops | bytes accessed | tf_op | source)
XLA Modules:
  0.0 177.5 jit_solution(3575578192846095971)
XLA Ops:
  7.2 0.7 all-gather.2.cloned.1.call-update
  7.9 0.3 copy-done
  8.3 1.4 convolution_convert_fusion.2
  9.7 1.2 broadcast_in_dim.204
  10.9 4.4 %all-to-all-start = ((bf16[8,384,256]{2,1,0:T(8,128)(2,1)}), bf16[8,384,256]{2,1,0:T(8,128)(2,1)S(1)}, u32[]{:S(2)}, u32[]{:S(2)}) async-start(bf16[8,384,256]{2,1,0:T(8,128)(2,1)} %broadcast_in_dim.204), calls=%async_computation | async-start | bytes 3145728 | tf_op jit(solution)/shard_map/all_to_all | solution.py:11
  15.3 26.5 %all_gather.6 = s32[6144,16]{0,1:T(8,128)S(1)} all-gather(s32[384,16]{0,1:T(8,128)S(1)} %pad_add_fusion), channel_id=1, replica_groups=mesh['expert'=16,'width'=8] {'expert'}, dimensions={0}, use_global_device_ids=true | all-gather | bytes 417792 | tf_op jit(solution)/shard_map/all_gather | solution.py:20
  41.9 0.2 fusion.49
  42.9 0.2 convert_reduce_fusion
  43.3 6.0 %select_reduce_fusion = (f32[384]{0:T(512)S(1)}, f32[384,8]{1,0:T(8,128)S(1)}) fusion(f32[384,256]{1,0:T(8,128)S(1)} %add_divide_fusion, s32[384,8]{1,0:T(8,128)S(1)} %copy.31), kind=kLoop, calls=%fused_computation.39 | loop fusion | flops 3142272 | bytes 419328 | tf_op jit(solution)/shard_map/reduce_sum | solution.py:49
  49.3 47.1 %all-gather.2.cloned.1.call-done = bf16[6144,896]{1,0:T(8,128)(2,1)} async-done(((bf16[384,896]{1,0:T(8,128)(2,1)}), bf16[6144,896]{1,0:T(8,128)(2,1)}) %all-gather.2.cloned.1.call-update) | async-done | bytes 11010064 | tf_op jit(solution)/shard_map/all_gather | solution.py:98
  96.5 7.6 %fusion.21 = bf16[16,192,896]{2,1,0:T(8,128)(2,1)S(1)} fusion(bf16[16,384,896]{2,1,0:T(8,128)(2,1)} %bitcast.21, s32[16,384]{1,0:T(8,128)S(1)} %eq.519, pred[16,384]{1,0:T(8,128)(4,1)S(1)} %and.314), kind=kOutput, calls=%fused_computation.41 | convolution fusion | flops 2119041024 | bytes 16545792 | tf_op jit(solution)/shard_map/sct,stw->scw/dot_general | solution.py:106
  104.1 1.8 fusion.1
  105.8 0.6 copy-done.1
  106.4 0.7 broadcast_in_dim.224
  107.1 4.3 %all-to-all-start.2 = ((f32[8,1,3072]{2,1,0:T(1,128)}), f32[8,1,3072]{2,1,0:T(1,128)S(1)}, u32[]{:S(2)}, u32[]{:S(2)}) async-start(f32[8,1,3072]{2,1,0:T(1,128)} %broadcast_in_dim.224), calls=%async_computation.2 | async-start | bytes 196608 | tf_op jit(solution)/shard_map/all_to_all | solution.py:11
  111.5 5.7 %all-to-all-done.2 = f32[8,1,3072]{2,1,0:T(1,128)S(1)} async-done(((f32[8,1,3072]{2,1,0:T(1,128)}), f32[8,1,3072]{2,1,0:T(1,128)S(1)}, u32[]{:S(2)}, u32[]{:S(2)}) %all-to-all-start.2) | async-done | bytes 98336 | tf_op jit(solution)/shard_map/all_to_all | solution.py:11
  117.3 0.7 all_to_all.23
  118.0 5.3 %all-to-all-start.3 = ((f32[16,192,1]{1,2,0:T(1,128)}), f32[16,192,1]{1,2,0:T(1,128)S(1)}, u32[]{:S(2)}, u32[]{:S(2)}) async-start(f32[16,192,1]{1,2,0:T(1,128)} %all_to_all.23), calls=%async_computation.3 | async-start | bytes 32768 | tf_op jit(solution)/shard_map/all_to_all | solution.py:112
  123.3 0.9 slice_reduce_fusion.6
  124.2 6.6 %all-to-all-done.3 = f32[16,192,1]{1,2,0:T(1,128)S(1)} async-done(((f32[16,192,1]{1,2,0:T(1,128)}), f32[16,192,1]{1,2,0:T(1,128)S(1)}, u32[]{:S(2)}, u32[]{:S(2)}) %all-to-all-start.3) | async-done | bytes 12320 | tf_op jit(solution)/shard_map/all_to_all | solution.py:112
  130.9 3.3 %fusion.15 = (f32[384]{0:T(512)S(1)}, f32[16,192]{1,0:T(8,128)S(1)}, f32[16,192]{1,0:T(8,128)S(1)}, f32[384]{0:T(512)S(1)}) fusion(f32[16,192]{1,0:T(8,128)S(1)} %bitcast.24, pred[192,384]{1,0:T(8,128)(4,1)S(1)} %get-tuple-element.62, pred[16,384]{1,0:T(8,128)(4,1)S(1)} %iota_compare_fusion.11, f32[384]{0:T(512)S(1)} %get-tuple-element.7, ...), kind=kLoop, calls=%fused_computation.33 | loop fusion | flops 11789568 | bytes 202752 | tf_op jit(solution)/shard_map/reduce_sum | solution.py:80
  134.1 9.4 %fusion.17 = (f32[384]{0:T(512)S(1)}, f32[16,192]{1,0:T(8,128)S(1)}, f32[16,192]{1,0:T(8,128)S(1)}, f32[384]{0:T(512)S(1)}, f32[16,192]{1,0:T(8,128)S(1)}, /*ind...) fusion(f32[16,192]{1,0:T(8,128)S(1)} %bitcast.25, ...), kind=kLoop, calls=%fused_computation.35 | loop fusion | flops 35368704 | bytes 583680 | tf_op jit(solution)/shard_map/reduce_sum | solution.py:80
  143.6 0.6 copy.32
  144.2 3.5 %all-to-all-start.1 = ((f32[16,192,1]{1,2,0:T(1,128)}), f32[16,192,1]{1,2,0:T(1,128)S(1)}, u32[]{:S(2)}, u32[]{:S(2)}) async-start(f32[16,192,1]{1,2,0:T(1,128)} %copy.32), calls=%async_computation.1 | async-start | bytes 32768 | tf_op jit(solution)/shard_map/all_to_all | solution.py:113
  148.3 2.2 %select_reduce_fusion.2 = bf16[384,256]{1,0:T(8,128)(2,1)S(1)} fusion(f32[384,8]{1,0:T(8,128)S(1)} %copy.37, s32[384,8]{1,0:T(8,128)S(1)} %copy.31), kind=kLoop, calls=%fused_computation.42 | loop fusion | flops 2260992 | bytes 221184 | tf_op jit(solution)/shard_map/reduce_sum | solution.py:58
  150.5 1.3 convolution_convert_fusion.1
  151.8 1.2 convolution_convert_fusion
  153.0 2.2 %all-to-all-done.1 = f32[16,192,1]{1,2,0:T(1,128)S(1)} async-done(((f32[16,192,1]{1,2,0:T(1,128)}), f32[16,192,1]{1,2,0:T(1,128)S(1)}, u32[]{:S(2)}, u32[]{:S(2)}) %all-to-all-start.1) | async-done | bytes 12320 | tf_op jit(solution)/shard_map/all_to_all | solution.py:113
  155.3 4.9 %all-to-all-start.4 = ((bf16[16,896,16]{1,2,0:T(8,128)(2,1)}), bf16[16,896,16]{1,2,0:T(8,128)(2,1)S(1)}, u32[]{:S(2)}, u32[]{:S(2)}) async-start(bf16[16,896,16]{1,2,0:T(8,128)(2,1)} %bitcast.5), calls=%async_computation.4 | async-start | bytes 917504 | tf_op jit(solution)/shard_map/all_to_all | solution.py:40
  160.3 6.0 %fusion = bf16[3072,896]{1,0:T(8,128)(2,1)} fusion(bf16[16,192,896]{2,1,0:T(8,128)(2,1)} %copy-done.1, f32[3072]{0:T(1024)S(1)} %mul.47), kind=kLoop, calls=%fused_computation.2 | loop fusion | flops 8257536 | bytes 11022336 | tf_op jit(solution)/shard_map/convert_element_type | solution.py:115
  166.3 3.6 %all-to-all-done.4 = bf16[16,896,16]{1,2,0:T(8,128)(2,1)S(1)} async-done(((bf16[16,896,16]{1,2,0:T(8,128)(2,1)}), bf16[16,896,16]{1,2,0:T(8,128)(2,1)S(1)}, u32[]{:S(2)}, u32[]{:S(2)}) %all-to-all-start.4) | async-done | bytes 458784 | tf_op jit(solution)/shard_map/all_to_all | solution.py:40
  169.9 0.7 convert_reduce_fusion.1
  (60 shorter events, 1.8 us)
Async XLA Ops:
  7.2 1.1 copy-start
  7.2 8.1 %copy-start.4 = (s32[384,8]{0,1:T(8,128)S(1)}, s32[384,8]{0,1:T(8,128)}, u32[]{:S(2)}) copy-start(s32[384,8]{0,1:T(8,128)} %param.11) | copy-start | bytes 36868
  7.2 8.1 %copy-start.3 = (s32[384,8]{0,1:T(8,128)S(1)}, s32[384,8]{0,1:T(8,128)}, u32[]{:S(2)}) copy-start(s32[384,8]{0,1:T(8,128)} %param.10) | copy-start | bytes 36868
  7.2 89.3 %all-gather.2.cloned.1.call-start = ((), (), s32[]{:S(2)}) async-start(), calls=%async_computation.5 | async-start | bytes 11698176 | tf_op jit(solution)/shard_map/all_gather | solution.py:98
  10.9 32.0 %all-to-all-start = ((bf16[8,384,256]{2,1,0:T(8,128)(2,1)}), bf16[8,384,256]{2,1,0:T(8,128)(2,1)S(1)}, u32[]{:S(2)}, u32[]{:S(2)}) async-start(bf16[8,384,256]{2,1,0:T(8,128)(2,1)} %broadcast_in_dim.204), calls=%async_computation | async-start | bytes 3145728 | tf_op jit(solution)/shard_map/all_to_all | solution.py:11
  43.3 60.7 %slice-start = ((s8[5505024]{0:T(1024)(128)(4,1)}), s8[1310720]{0:T(1024)(128)(4,1)S(1)}, s32[]{:S(2)}) async-start(s8[5505024]{0:T(1024)(128)(4,1)} %bitcast.22), calls=%async_computation.6 | async-start | bytes 2621440
  96.5 7.6 %slice-start.1 = ((s8[5505024]{0:T(1024)(128)(4,1)}), s8[4194304]{0:T(1024)(128)(4,1)S(1)}, s32[]{:S(2)}) async-start(s8[5505024]{0:T(1024)(128)(4,1)} %bitcast.22), calls=%async_computation.7 | async-start | bytes 8388608
  104.0 2.4 %copy-start.1 = (bf16[16,192,896]{2,1,0:T(8,128)(2,1)}, bf16[16,192,896]{2,1,0:T(8,128)(2,1)S(1)}, u32[]{:S(2)}) copy-start(bf16[16,192,896]{2,1,0:T(8,128)(2,1)S(1)} %fusion.21) | copy-start | bytes 16515076
  106.4 45.4 %copy-start.2 = (bf16[896,256]{1,0:T(8,128)(2,1)S(1)}, bf16[896,256]{1,0:T(8,128)(2,1)}, u32[]{:S(2)}) copy-start(bf16[896,256]{1,0:T(8,128)(2,1)} %param.8) | copy-start | bytes 1376260
  107.1 10.1 %all-to-all-start.2 = ((f32[8,1,3072]{2,1,0:T(1,128)}), f32[8,1,3072]{2,1,0:T(1,128)S(1)}, u32[]{:S(2)}, u32[]{:S(2)}) async-start(f32[8,1,3072]{2,1,0:T(1,128)} %broadcast_in_dim.224), calls=%async_computation.2 | async-start | bytes 196608 | tf_op jit(solution)/shard_map/all_to_all | solution.py:11
  118.0 12.9 %all-to-all-start.3 = ((f32[16,192,1]{1,2,0:T(1,128)}), f32[16,192,1]{1,2,0:T(1,128)S(1)}, u32[]{:S(2)}, u32[]{:S(2)}) async-start(f32[16,192,1]{1,2,0:T(1,128)} %all_to_all.23), calls=%async_computation.3 | async-start | bytes 32768 | tf_op jit(solution)/shard_map/all_to_all | solution.py:112
  144.2 11.0 %all-to-all-start.1 = ((f32[16,192,1]{1,2,0:T(1,128)}), f32[16,192,1]{1,2,0:T(1,128)S(1)}, u32[]{:S(2)}, u32[]{:S(2)}) async-start(f32[16,192,1]{1,2,0:T(1,128)} %copy.32), calls=%async_computation.1 | async-start | bytes 32768 | tf_op jit(solution)/shard_map/all_to_all | solution.py:113
  155.3 14.7 %all-to-all-start.4 = ((bf16[16,896,16]{1,2,0:T(8,128)(2,1)}), bf16[16,896,16]{1,2,0:T(8,128)(2,1)S(1)}, u32[]{:S(2)}, u32[]{:S(2)}) async-start(bf16[16,896,16]{1,2,0:T(8,128)(2,1)} %bitcast.5), calls=%async_computation.4 | async-start | bytes 917504 | tf_op jit(solution)/shard_map/all_to_all | solution.py:40
Sparse Core Ops, SparseCore 0:
  10.2 86.2 all-gather.1
where the time goes:
time: 178 us; the launch traced here: 177 us
  waiting for transfers between devices  66 us (37%)
  other arithmetic  30.9 us (17%)
  blocking collectives  26.5 us (15%)
  starting transfers between devices  22.4 us (13%)
  between operations  14.5 us (8%)
  matrix products  11.4 us (6%)
  local copies, waits for them, and re-layouts  5.78 us (3%)
    all_gather x1, waiting for transfers between devices, body(): all_grads = lax.all_gather(out_grad, 'expert', axis=0, tiled=True)  47.1 us
    all_gather x1, blocking collectives, sent_together(): lax.all_gather(both, axis, axis=dim, tiled=True)  26.5 us
    reduce_sum x2, other arithmetic, collect_values(): jnp.sum(jnp.where(table, grid[:, :, None], 0.0), axis=(0, 1))  12.7 us
    all_to_all x2, starting transfers between devices, copy_for_each(): lax.all_to_all(jnp.broadcast_to(x[None], (length, *x.shape)), axis, 0, 0,...  8.67 us
    dot_general x1, matrix products, body(): jnp.einsum('sct,stw->scw', routing, grads_grid, preferred_element_type=jn...  7.56 us
    all_to_all x1, waiting for transfers between devices, body(): lax.all_to_all(dot_totals, 'expert', split_axis=0, concat_axis=0, tiled=T...  6.64 us
    reduce_sum x1, other arithmetic, gate_parts(): totals = jnp.sum(picked, axis=1, keepdims=True)  6.04 us
    convert_element_type x1, other arithmetic, body(): (gate_values[:, None] * received.astype(jnp.float32)).astype(jnp.bfloat16)  5.98 us
  transfers between devices with their start and end apart: 6, of which 5 were waited for; matrix products, arithmetic and copies ran while one was open for 13% of the time, Pallas kernels for 0%

commit v1 on v0

v1 whole, which is shorter than its diff:
```python
import functools

import jax
import jax.numpy as jnp
from jax import lax
from jax.experimental import pallas as pl
from jax.experimental.pallas import tpu as pltpu
from jax.sharding import PartitionSpec as P

MESH = pl.DeviceIdType.MESH
SIDE = 4
PER_DEV = 16
ROUTE_SCALE = 2.5
ROW = 256
BF16, F32, I32 = jnp.bfloat16, jnp.float32, jnp.int32
NT = (((1,), (1,)), ((), ()))


def kernel(
    tok_hbm, grad_hbm, weight_hbm, eo_hbm, ids_ref, slots_ref,
    eg_hbm, rg_ref, ig_ref,
    x0, x1, rs0, rs1, rl0, rl1, tok, weight, eo, egv, oh,
    tb_own, tb_in0, tb_in1, tbf0, tbf1, slot_own, eloc, lsend, win, gsend, gin, dsend, rin, win2,
    ggv, picked_v, lgt32, lgt, rb, rr,
    in_sem, eg_sem,
    xs, xr, tbs, tbr, ws, wr, gs, gr, ss, sr, rls, rlr, rts, rtr, w2s, w2r, rps, rpr,
):
    n = lax.axis_size("expert")
    n_width = lax.axis_size("width")
    me = lax.axis_index("expert")
    mw = lax.axis_index("width")
    top, t_rows = ids_ref.shape
    cap = rs0.shape[1]
    half, t_half = cap // 2, t_rows // 2
    xs_of, rs_of, rl_of = (x0, x1), (rs0, rs1), (rl0, rl1)
    tb_in, tbf = (tb_in0, tb_in1), (tbf0, tbf1)
    c0 = x0.shape[2]
    cols = ((0, c0), (c0, x1.shape[2]))
    core = lax.rem(mw, 2)
    gy, gz = me // SIDE, lax.rem(me, SIDE)

    flip = (core, 1 - core)
    p1 = tuple(gz + f * (gy - gz) for f in flip)
    p2 = tuple(gy + f * (gz - gy) for f in flip)

    def mod(v):
        return lax.rem(v + 2 * SIDE, SIDE)

    def place(g, a1, a2):
        return mod(a1) * (1 + (SIDE - 1) * flip[g]) + mod(a2) * (SIDE - (SIDE - 1) * flip[g])

    def ring1(g, step):
        return place(g, p1[g] + step, p2[g])

    def ring2(g, step):
        return place(g, p1[g], p2[g] + step)

    def to(src, dst, send, recv, e=None, w=None):
        where = {"expert": me if e is None else e, "width": mw if w is None else w}
        return pltpu.make_async_remote_copy(
            src_ref=src, dst_ref=dst, send_sem=send, recv_sem=recv, device_id=where, device_id_type=MESH
        )

    barrier = pltpu.get_barrier_semaphore()

    def greet_expert(o, carry):
        pl.semaphore_signal(
            barrier, inc=1, device_id={"expert": lax.rem(me + o, n), "width": mw}, device_id_type=MESH
        )
        return carry

    def greet_width(o, carry):
        pl.semaphore_signal(
            barrier, inc=1, device_id={"expert": me, "width": lax.rem(mw + o, n_width)}, device_id_type=MESH
        )
        return carry

    lax.fori_loop(1, n, greet_expert, 0)
    lax.fori_loop(1, n_width, greet_width, 0)

    loads = [
        pltpu.make_async_copy(grad_hbm.at[:, pl.ds(cols[g][0], cols[g][1])], xs_of[g].at[0], in_sem.at[g])
        for g in range(2)
    ]
    loads.append(pltpu.make_async_copy(tok_hbm, tok, in_sem.at[2]))
    loads.append(pltpu.make_async_copy(weight_hbm, weight, in_sem.at[3]))
    loads.append(pltpu.make_async_copy(eo_hbm, eo, in_sem.at[4]))
    for load in loads:
        load.start()

    row16 = lax.broadcasted_iota(I32, (n, t_rows), 0)
    slot_tbl = jnp.full((n, t_rows), -1, I32)
    eloc_tbl = jnp.full((n, t_rows), -1, I32)
    for k in range(top):
        ids = ids_ref[k : k + 1, :]
        dev = lax.shift_right_logical(ids, 4)
        hit = row16 == dev
        slot_tbl = jnp.where(hit, slots_ref[k : k + 1, :], slot_tbl)
        eloc_tbl = jnp.where(hit, ids - dev * PER_DEV, eloc_tbl)
    slot_own[...] = slot_tbl
    eloc[...] = eloc_tbl
    slot_f = slot_tbl.astype(F32)
    tbf0[0] = slot_f
    tbf1[0] = slot_f
    tb_own[...] = slot_f.astype(BF16)
    dsend[...] = jnp.zeros_like(dsend)

    pl.semaphore_wait(barrier, n - 1 + n_width - 1)

    def first_copy(g, k):
        step, h = ((1, 0), (1, 1), (-1, 1), (-1, 0))[k]
        rows = pl.ds(h * t_half, t_half)
        return to(
            xs_of[g].at[0, rows], xs_of[g].at[step % SIDE, rows], xs.at[g, k], xr.at[g, k], e=ring1(g, step)
        )

    def onward_copy(g, k):
        step, h = ((1, 0), (-1, 1))[k]
        rows = pl.ds(h * t_half, t_half)
        return to(
            xs_of[g].at[step % SIDE, rows], xs_of[g].at[2, rows], xs.at[g, 4 + k], xr.at[g, 4 + k], e=ring1(g, step)
        )

    def table_copy(g, j):
        return to(tb_own, tb_in[g].at[j], tbs.at[g, j], tbr.at[g, j], e=ring1(g, j))

    for g in range(2):
        loads[g].wait()
        first_copy(g, 0).start()
        first_copy(g, 2).start()
    for g in range(2):
        for j in (1, 3, 2):
            table_copy(g, j).start()
    for g in range(2):
        first_copy(g, 1).start()
        first_copy(g, 3).start()

    loads[2].wait()
    loads[3].wait()
    logits_t = jnp.dot(tok[...], weight[...], preferred_element_type=F32).T
    for d in range(n):
        block = logits_t[d * PER_DEV : (d + 1) * PER_DEV, :]
        hit = row16[:PER_DEV] == eloc_tbl[d : d + 1, :]
        lsend[d : d + 1, :] = jnp.sum(jnp.where(hit, block, 0.0), axis=0, keepdims=True)

    slot_iota = lax.broadcasted_iota(I32, (ROW, t_rows), 0).astype(F32)

    def own_table(d, carry):
        row = tbf0[0, pl.ds(d, 1), :]
        oh[d] = jnp.where(row == slot_iota, 1.0, 0.0).astype(BF16)
        return carry

    lax.fori_loop(0, n, own_table, 0)
    win[mw] = lsend[...]

    def logit_copy(o):
        return to(lsend, win.at[mw], ws.at[o], wr.at[o], w=lax.rem(mw + o, n_width))

    def send_logits(o, carry):
        logit_copy(o).start()
        return carry

    lax.fori_loop(1, n_width, send_logits, 0)

    cap_iota = lax.broadcasted_iota(I32, (cap, t_rows), 0).astype(F32)

    def select(g, j0, step, count):
        def one(i, carry):
            j, m = j0 + step * (i // SIDE), lax.rem(i, SIDE)
            row = tbf[g][j, pl.ds(ring2(g, m), 1), :]
            pick = jnp.where(row == cap_iota, 1.0, 0.0).astype(BF16)
            rows = jnp.dot(pick, xs_of[g][j], preferred_element_type=F32).astype(BF16)
            away = (m + SIDE - 1) // SIDE
            home = place(g, p1[g] - j, p2[g])
            rs_of[g][home * (1 - away) + away * (n + j * SIDE + m)] = rows
            return carry

        lax.fori_loop(0, count * SIDE, one, 0)

    def direct_copy(g, j, kind):
        m = (1, 3)[kind]
        return to(
            rs_of[g].at[n + j * SIDE + m], rs_of[g].at[place(g, p1[g] - j, p2[g])],
            ss.at[g, j, kind], sr.at[g, j, kind], e=ring2(g, (1, -1)[kind]),
        )

    def relay_copy(g, j, h):
        return to(
            rs_of[g].at[n + j * SIDE + 2, pl.ds(h * half, half)], rl_of[g].at[j, h],
            ss.at[g, j, 2 + h], rlr.at[g, j, h], e=ring2(g, (1, -1)[h]),
        )

    def final_copy(g, j, h):
        step = (1, -1)[h]
        return to(
            rl_of[g].at[j, h], rs_of[g].at[place(g, p1[g] - j, p2[g] - step), pl.ds(h * half, half)],
            rls.at[g, j, h], sr.at[g, j, 2 + h], e=ring2(g, step),
        )

    def send_picked(j):
        for g in range(2):
            relay_copy(g, j, 0).start()
            relay_copy(g, j, 1).start()
        for g in range(2):
            direct_copy(g, j, 0).start()
            direct_copy(g, j, 1).start()

    def pass_on(j):
        for g in range(2):
            for h in range(2):
                relay_copy(g, j, h).wait_recv()
                final_copy(g, j, h).start()

    for g in range(2):
        select(g, 0, 0, 1)
    for k in range(2):
        for g in range(2):
            first_copy(g, 2 * k).wait_recv()
            onward_copy(g, k).start()
    send_picked(0)

    def wait_logits(o, carry):
        to(lsend, win.at[lax.rem(mw + n_width - o, n_width)], ws.at[o], wr.at[o], w=mw).wait_recv()
        return carry

    lax.fori_loop(1, n_width, wait_logits, 0)
    total_logits = win[0]
    for w in range(1, win.shape[0]):
        total_logits = total_logits + win[w]
    picked = jnp.where(eloc_tbl >= 0, jax.nn.sigmoid(total_logits), 0.0)
    picked_v[...] = picked
    gates = (ROUTE_SCALE * picked / jnp.sum(picked, axis=0, keepdims=True)).astype(BF16).astype(F32)

    def gate_row(d, acc):
        only = jnp.where(row16 == d, gates, 0.0).astype(BF16)
        return acc + lax.dot_general(only, oh[d], NT, preferred_element_type=F32)

    gate_slots = lax.fori_loop(0, n, gate_row, jnp.zeros((n, ROW), F32))
    for d in range(n):
        gsend[d] = gate_slots[d : d + 1, :]
    gin[me] = gsend[me]

    def gate_copy(o):
        d = lax.rem(me + o, n)
        return to(gsend.at[d], gin.at[me], gs.at[o], gr.at[o], e=d)

    def send_gates(o, carry):
        gate_copy(o).start()
        return carry

    lax.fori_loop(1, n, send_gates, 0)

    def take_tables(js):
        for g in range(2):
            for j in js:
                table_copy(g, j).wait_recv()
                tbf[g][j] = tb_in[g][j].astype(F32)

    take_tables((1, 3))
    for g in range(2):
        first_copy(g, 1).wait_recv()
        first_copy(g, 3).wait_recv()
        select(g, 1, 2, 2)
    send_picked(1)
    send_picked(3)
    take_tables((2,))
    for g in range(2):
        onward_copy(g, 0).wait_recv()
        onward_copy(g, 1).wait_recv()
        select(g, 2, 0, 1)
    send_picked(2)

    loads[4].wait()

    def wait_gates(o, carry):
        to(gsend.at[0], gin.at[lax.rem(me + n - o, n)], gs.at[o], gr.at[o], e=me).wait_recv()
        return carry

    lax.fori_loop(1, n, wait_gates, 0)

    ones = jnp.ones((8, 128), BF16)
    eye = lax.broadcasted_iota(I32, (cap, cap), 0) == lax.broadcasted_iota(I32, (cap, cap), 1)

    def offsets_of(o1, o2):
        return place(0, p1[0] - o1, p2[0] - o2)

    def return_copy(s):
        o = lax.rem(me + n - s, n)
        return to(dsend.at[s], rin.at[me], rts.at[o], rtr.at[o], e=s)

    def out_copy(s):
        return pltpu.make_async_copy(egv.at[s], eg_hbm.at[s], eg_sem.at[s])

    def gate_grads_of(s):
        acc = None
        for g in range(2):
            for at in range(0, cols[g][1], 128):
                a = rs_of[g][s, :, at : at + 128].astype(F32)
                b = eo[s, :, cols[g][0] + at : cols[g][0] + at + 128].astype(F32)
                acc = a * b if acc is None else acc + a * b
        high = acc.astype(BF16)
        low = (acc - high.astype(F32)).astype(BF16)
        dots = lax.dot_general(ones, high, NT, preferred_element_type=F32)
        dots = dots + lax.dot_general(ones, low, NT, preferred_element_type=F32)
        dsend[s, :, :cap] = dots[0:1, :]

    def expert_grad_of(s):
        scale = jnp.where(eye, gin[s][:, :cap], 0.0).astype(BF16)
        for g in range(2):
            value = jnp.dot(scale, rs_of[g][s], preferred_element_type=F32)
            egv[s, :, cols[g][0] : cols[g][0] + cols[g][1]] = value.astype(BF16)
        out_copy(s).start()

    def arrived(o1, o2):
        for g, j, by in ((0, o1, o2), (1, o2, o1)):
            if by == 1:
                direct_copy(g, j, 0).wait_recv()
            elif by == 3:
                direct_copy(g, j, 1).wait_recv()
            elif by == 2:
                final_copy(g, j, 0).wait_recv()
                final_copy(g, j, 1).wait_recv()

    def blocks(count, offset, listed):
        for o1, o2 in listed:
            arrived(o1, o2)

        def one(i, carry):
            s = offsets_of(*offset(i))
            gate_grads_of(s)
            expert_grad_of(s)
            return_copy(s).start()
            return carry

        lax.fori_loop(0, count, one, 0)

    def one_axis(i):
        q, r = i // 2, 1 + 2 * lax.rem(i, 2)
        return q * r, (1 - q) * r

    def both_near(i):
        return 1 + 2 * (i // 2), 1 + 2 * lax.rem(i, 2)

    def one_far(i):
        q, r = i // 2, 1 + 2 * lax.rem(i, 2)
        return 2 * q + (1 - q) * r, q * r + 2 * (1 - q)

    gate_grads_of(me)
    expert_grad_of(me)
    rin[me] = dsend[me]
    blocks(4, one_axis, [(0, 1), (0, 3), (1, 0), (3, 0)])
    pass_on(0)
    pass_on(1)
    blocks(4, both_near, [(1, 1), (1, 3), (3, 1), (3, 3)])
    pass_on(3)
    pass_on(2)
    blocks(2, lambda i: (2 * i, 2 - 2 * i), [(0, 2), (2, 0)])
    blocks(4, one_far, [(1, 2), (3, 2), (2, 1), (2, 3)])
    arrived(2, 2)
    last = offsets_of(2, 2)
    gate_grads_of(last)
    expert_grad_of(last)
    return_copy(last).start()

    def wait_return(o, carry):
        to(dsend.at[0], rin.at[lax.rem(me + o, n)], rts.at[o], rtr.at[o], e=me).wait_recv()
        return carry

    lax.fori_loop(1, n, wait_return, 0)

    def width_copy(o):
        return to(rin, win2.at[mw], w2s.at[o], w2r.at[o], w=lax.rem(mw + o, n_width))

    def send_width(o, carry):
        width_copy(o).start()
        return carry

    lax.fori_loop(1, n_width, send_width, 0)
    win2[mw] = rin[...]

    def wait_width(o, carry):
        to(rin, win2.at[lax.rem(mw + n_width - o, n_width)], w2s.at[o], w2r.at[o], w=mw).wait_recv()
        return carry

    lax.fori_loop(1, n_width, wait_width, 0)
    for d in range(n):
        row = win2[0, d]
        for w in range(1, win2.shape[0]):
            row = row + win2[w, d]
        ggv[d : d + 1, :] = row

    slots = slot_own[...]
    lane = jnp.bitwise_and(slots, 127)
    pieces = []
    for at in range(0, t_rows, 128):
        index = lane[:, at : at + 128]
        low = jnp.take_along_axis(ggv[:, 0:128], index, axis=1)
        high = jnp.take_along_axis(ggv[:, 128:256], index, axis=1)
        pieces.append(jnp.where(slots[:, at : at + 128] < 128, low, high))
    chosen = slots >= 0
    gate_grads = jnp.where(chosen, jnp.concatenate(pieces, axis=1), 0.0)

    picked = picked_v[...]
    totals = jnp.sum(picked, axis=0, keepdims=True)
    weighted = jnp.sum(gate_grads * picked, axis=0, keepdims=True) / totals
    local = jnp.where(chosen, ROUTE_SCALE / totals * (gate_grads - weighted) * picked * (1.0 - picked), 0.0)
    for d in range(n):
        hit = row16[:PER_DEV] == eloc[d : d + 1, :]
        block = jnp.where(hit, local[d : d + 1, :], 0.0)
        lgt32[d * PER_DEV : (d + 1) * PER_DEV, :] = block
        lgt[d * PER_DEV : (d + 1) * PER_DEV, :] = block.astype(BF16)

    part = jnp.dot(lgt[...], tok[...], preferred_element_type=F32)
    rb[...] = part.astype(BF16).reshape(rb.shape)

    def part_copy(o):
        d = lax.rem(me + o, n)
        return to(rb.at[d], rr.at[me], rps.at[o], rpr.at[o], e=d)

    def send_part(o, carry):
        part_copy(o).start()
        return carry

    logit_grads = lgt32[...].T.astype(BF16)
    lax.fori_loop(1, n, send_part, 0)
    rr[me] = rb[me]
    ig_ref[...] = lax.dot_general(logit_grads, weight[...], NT, preferred_element_type=F32).astype(BF16)

    def wait_part(o, carry):
        to(rb.at[0], rr.at[lax.rem(me + n - o, n)], rps.at[o], rpr.at[o], e=me).wait_recv()
        return carry

    lax.fori_loop(1, n, wait_part, 0)
    total = rr[0].astype(F32)
    for d in range(1, n):
        total = total + rr[d].astype(F32)
    rg_ref[...] = total

    for g in range(2):
        for k in range(4):
            first_copy(g, k).wait_send()
        for k in range(2):
            onward_copy(g, k).wait_send()
        for j in range(1, SIDE):
            table_copy(g, j).wait_send()
        for j in range(SIDE):
            for h in range(2):
                direct_copy(g, j, h).wait_send()
                relay_copy(g, j, h).wait_send()
                final_copy(g, j, h).wait_send()

    def width_sent(o, carry):
        logit_copy(o).wait_send()
        width_copy(o).wait_send()
        return carry

    def expert_sent(o, carry):
        gate_copy(o).wait_send()
        part_copy(o).wait_send()
        return_copy(lax.rem(me + n - o, n)).wait_send()
        return carry

    def written(s, carry):
        out_copy(s).wait()
        return carry

    lax.fori_loop(1, n_width, width_sent, 0)
    lax.fori_loop(1, n, expert_sent, 0)
    lax.fori_loop(0, n, written, 0)


def body(tokens_in, out_grad, router_weight, expert_out, expert_ids, slot_ids):
    n = lax.axis_size("expert")
    n_width = lax.axis_size("width")
    t_rows, d_cols = out_grad.shape
    top = expert_ids.shape[1]
    experts = router_weight.shape[1]
    cap = t_rows * top // n
    c0 = (d_cols // 128 + 1) // 2 * 128
    c1 = d_cols - c0
    hbm, vmem = pl.BlockSpec(memory_space=pl.ANY), pl.BlockSpec(memory_space=pltpu.VMEM)
    dma = pltpu.SemaphoreType.DMA
    scratch = [
        pltpu.VMEM((SIDE, t_rows, c0), BF16),
        pltpu.VMEM((SIDE, t_rows, c1), BF16),
        pltpu.VMEM((2 * n, cap, c0), BF16),
        pltpu.VMEM((2 * n, cap, c1), BF16),
        pltpu.VMEM((SIDE, 2, cap // 2, c0), BF16),
        pltpu.VMEM((SIDE, 2, cap // 2, c1), BF16),
        pltpu.VMEM((t_rows, d_cols), BF16),
        pltpu.VMEM((d_cols, experts), BF16),
        pltpu.VMEM((n, cap, d_cols), BF16),
        pltpu.VMEM((n, cap, d_cols), BF16),
        pltpu.VMEM((n, ROW, t_rows), BF16),
        pltpu.VMEM((n, t_rows), BF16),
        pltpu.VMEM((SIDE, n, t_rows), BF16),
        pltpu.VMEM((SIDE, n, t_rows), BF16),
        pltpu.VMEM((SIDE, n, t_rows), F32),
        pltpu.VMEM((SIDE, n, t_rows), F32),
        pltpu.VMEM((n, t_rows), I32),
        pltpu.VMEM((n, t_rows), I32),
        pltpu.VMEM((n, t_rows), F32),
        pltpu.VMEM((n_width, n, t_rows), F32),
        pltpu.VMEM((n, 1, ROW), F32),
        pltpu.VMEM((n, 1, ROW), F32),
        pltpu.VMEM((n, 1, ROW), F32),
        pltpu.VMEM((n, 1, ROW), F32),
        pltpu.VMEM((n_width, n, 1, ROW), F32),
        pltpu.VMEM((n, ROW), F32),
        pltpu.VMEM((n, t_rows), F32),
        pltpu.VMEM((experts, t_rows), F32),
        pltpu.VMEM((experts, t_rows), BF16),
        pltpu.VMEM((n, experts // n, d_cols), BF16),
        pltpu.VMEM((n, experts // n, d_cols), BF16),
        dma((5,)),
        dma((n,)),
        dma((2, 6)), dma((2, 6)),
        dma((2, SIDE)), dma((2, SIDE)),
        dma((n_width,)), dma((n_width,)),
        dma((n,)), dma((n,)),
        dma((2, SIDE, 4)), dma((2, SIDE, 4)),
        dma((2, SIDE, 2)), dma((2, SIDE, 2)),
        dma((n,)), dma((n,)),
        dma((n_width,)), dma((n_width,)),
        dma((n,)), dma((n,)),
    ]
    expert_grad, router_grad, input_grad = pl.pallas_call(
        kernel,
        out_shape=(
            jax.ShapeDtypeStruct((n, cap, d_cols), BF16),
            jax.ShapeDtypeStruct((experts // n, d_cols), F32),
            jax.ShapeDtypeStruct((t_rows, d_cols), BF16),
        ),
        in_specs=[hbm, hbm, hbm, hbm, vmem, vmem],
        out_specs=(hbm, vmem, vmem),
        scratch_shapes=scratch,
        compiler_params=pltpu.CompilerParams(
            collective_id=0, has_side_effects=True, vmem_limit_bytes=60 * 1024 * 1024
        ),
    )(
        tokens_in, out_grad, router_weight, expert_out.reshape(n, cap, d_cols), expert_ids.T, slot_ids.T
    )
    return expert_grad.reshape(n * cap, d_cols), router_grad.T, input_grad


def solution(mesh):
    return jax.shard_map(
        body,
        mesh=mesh,
        in_specs=(
            P("expert", "width"),
            P("expert", "width"),
            P("width", None),
            P("expert", "width"),
            P("expert", None),
            P("expert", None),
        ),
        out_specs=(P("expert", "width"), P("width", "expert"), P("expert", "width")),
        check_vma=False,
    )
```

time: 178 us -> 81.3 us (0.46)
  Pallas kernels: 0 us -> 73.4 us
  waiting for transfers between devices: 66 us -> 0 us
  other arithmetic: 30.9 us -> 0 us
  blocking collectives: 26.5 us -> 0 us
  starting transfers between devices: 22.4 us -> 0 us
  between operations: 14.5 us -> 0.66 us
  matrix products: 11.4 us -> 0 us
    pallas_call x0 -> x1, Pallas kernels: none -> 73.4 us  [body(): pl.pallas_call(kernel, out_shape=(jax.ShapeDtypeStruct((n, cap, d_cols),...]
    all_gather x1 -> x0, waiting for transfers between devices: 47.1 us -> none  [body(): all_grads = lax.all_gather(out_grad, 'expert', axis=0, tiled=True)]
    all_gather x1 -> x0, blocking collectives: 26.5 us -> none  [sent_together(): lax.all_gather(both, axis, axis=dim, tiled=True)]
    all_to_all x5 -> x0, starting transfers between devices: 22.4 us -> none  [the longest x2 8.67 us: copy_for_each(): lax.all_to_all(jnp.broadcast_to(x[None], (length, *x.shape)), axis, 0, 0,...]
    reduce_sum x9 -> x0, other arithmetic: 22.2 us -> none  [the longest x2 12.7 us: collect_values(): jnp.sum(jnp.where(table, grid[:, :, None], 0.0), axis=(0, 1))]
    all_to_all x5 -> x0, waiting for transfers between devices: 18.2 us -> none  [the longest x1 6.64 us: body(): lax.all_to_all(dot_totals, 'expert', split_axis=0, concat_axis=0, tiled=T...]
    dot_general x4 -> x0, matrix products: 11.4 us -> none  [the longest x1 7.56 us: body(): jnp.einsum('sct,stw->scw', routing, grads_grid, preferred_element_type=jn...]
    convert_element_type x2 -> x0, other arithmetic: 6.1 us -> none  [the longest x1 5.98 us: body(): (gate_values[:, None] * received.astype(jnp.float32)).astype(jnp.bfloat16)]
  transfers between devices with their start and end apart: 6 -> 0, of which waited for: 5 -> 0; matrix products, arithmetic and copies ran while one was open for 13% -> 0% of each run, Pallas kernels for 0% -> 0%
where the time goes in v1:
time: 81.3 us; the launch traced here: 81 us
  Pallas kernels  73.4 us (90%)
  local copies, waits for them, and re-layouts  6.99 us (9%)
    pallas_call x1, Pallas kernels, body(): pl.pallas_call(kernel, out_shape=(jax.ShapeDtypeStruct((n, cap, d_cols),...  73.4 us
    unnamed x7, local copies, waits for them, and re-layouts  6.99 us

profile of v1, /device:TPU:0, one launch (start us, length us, event | category | flops | bytes accessed | tf_op | source)
XLA Modules:
  0.0 81.0 jit_solution(12623543864642550615)
XLA Ops:
  0.6 73.4 %shard_map.85 = (bf16[16,192,896]{2,1,0:T(8,128)(2,1)}, f32[16,896]{1,0:T(8,128)}, bf16[384,896]{1,0:T(8,128)(2,1)}) custom-call(bf16[384,896]{1,0:T(8,128)(2,1)} %tok_hbm.1, bf16[384,896]{1,0:T(8,128)(2,1)} %grad_hbm.1, bf16[896,256]{1,0:T(8,128)(2,1)} %weight_hbm.1, bf16[16,192,896]{2,1,0:T(8,128)(2,1)} %bitcast.6, s32[8,384]{1,0:T(8,128)} %bitcast.8, ...), custom_call_target="tpu_custom_call" | custom-call | tf_op jit(solution)/shard_map/pallas_call | solution.py:527
  74.0 0.0 copy-start.1
  74.0 0.0 copy-start
  74.0 5.5 %copy.12 = bf16[3072,896]{1,0:T(8,128)(2,1)} copy(bf16[3072,896]{1,0:T(8,128)(2,1)} %bitcast.5) | data formatting | bytes 11010048
  79.5 0.0 copy-done.1
  79.5 0.6 copy.13
  80.2 0.0 copy-done
  80.2 0.8 %copy.14 = bf16[384,896]{1,0:T(8,128)(2,1)} copy(bf16[384,896]{1,0:T(8,128)(2,1)S(1)} %copy-done) | data formatting | bytes 1376256
Async XLA Ops:
  74.0 5.5 %copy-start.1 = (f32[16,896]{1,0:T(8,128)S(1)}, f32[16,896]{1,0:T(8,128)}, u32[]{:S(2)}) copy-start(f32[16,896]{1,0:T(8,128)} %get-tuple-element.7) | copy-start | bytes 172036
  74.0 6.2 %copy-start = (bf16[384,896]{1,0:T(8,128)(2,1)S(1)}, bf16[384,896]{1,0:T(8,128)(2,1)}, u32[]{:S(2)}) copy-start(bf16[384,896]{1,0:T(8,128)(2,1)} %get-tuple-element.14) | copy-start | bytes 2064388

commit v2 on v1

v2 whole, which is shorter than its diff:
```python
import functools

import jax
import jax.numpy as jnp
from jax import lax
from jax.experimental import pallas as pl
from jax.experimental.pallas import tpu as pltpu
from jax.sharding import PartitionSpec as P

MESH = pl.DeviceIdType.MESH
SIDE = 4
PER_DEV = 16
ROUTE_SCALE = 2.5
ROW = 256
BF16, F32, I32 = jnp.bfloat16, jnp.float32, jnp.int32
NT = (((1,), (1,)), ((), ()))


SELF = ((0, 0),)
FAR_ONE = ((0, 2), (2, 0))
FAR_BOTH = ((2, 2),)
FAR_NEAR = ((1, 2), (3, 2), (2, 1), (2, 3))
DIAGONAL = ((1, 1), (1, 3), (3, 1), (3, 3))
BESIDE = ((0, 1), (0, 3), (1, 0), (3, 0))
OFFSETS = SELF + FAR_ONE + FAR_BOTH + FAR_NEAR + DIAGONAL + BESIDE
EARLY, MIDDLE, LATE = 8, 4, 4


def kernel(
    tok_hbm, grad_hbm, weight_hbm, eo_hbm, ids_hbm, slots_hbm,
    egv, rg_ref, ig_ref,
    x0, x1, rs0, rs1, tok, weight, eo, ids_ref, slots_ref, oh,
    tb_own, tb_in0, tb_in1, tbf0, tbf1, slot_own, eloc, lsend, win, gsend, gin, dsend, rin, win2,
    ggv, picked_v, lgt32, lgt, rb, rr,
    in_sem, xs, xr, tbs, tbr, ws, wr, gs, gr, ss, sr, rts, rtr, w2s, w2r, rps, rpr,
):
    n = lax.axis_size("expert")
    n_width = lax.axis_size("width")
    me = lax.axis_index("expert")
    mw = lax.axis_index("width")
    top, t_rows = ids_ref.shape
    cap = rs0.shape[1]
    t_half = t_rows // 2
    xs_of, rs_of = (x0, x1), (rs0, rs1)
    tb_in, tbf = (tb_in0, tb_in1), (tbf0, tbf1)
    c0 = x0.shape[2]
    cols = ((0, c0), (c0, x1.shape[2]))
    core = lax.rem(mw, 2)
    gy, gz = me // SIDE, lax.rem(me, SIDE)

    flip = (core, 1 - core)
    p1 = tuple(gz + f * (gy - gz) for f in flip)
    p2 = tuple(gy + f * (gz - gy) for f in flip)

    def mod(v):
        return lax.rem(v + 2 * SIDE, SIDE)

    def place(g, a1, a2):
        return mod(a1) * (1 + (SIDE - 1) * flip[g]) + mod(a2) * (SIDE - (SIDE - 1) * flip[g])

    def ring1(g, step):
        return place(g, p1[g] + step, p2[g])

    def ring2(g, step):
        return place(g, p1[g], p2[g] + step)

    def target(dy, dz):
        return mod(gy + dy) * SIDE + mod(gz + dz)

    def origin(dy, dz):
        return mod(gy - dy) * SIDE + mod(gz - dz)

    def to(src, dst, send, recv, e=None, w=None):
        where = {"expert": me if e is None else e, "width": mw if w is None else w}
        return pltpu.make_async_remote_copy(
            src_ref=src, dst_ref=dst, send_sem=send, recv_sem=recv, device_id=where, device_id_type=MESH
        )

    def await_recv(like, sem):
        to(like, like, sem, sem).wait_recv()

    def await_sent(like, sem):
        to(like, like, sem, sem).wait_send()

    barrier = pltpu.get_barrier_semaphore()

    def greet_expert(o, carry):
        pl.semaphore_signal(
            barrier, inc=1, device_id={"expert": lax.rem(me + o, n), "width": mw}, device_id_type=MESH
        )
        return carry

    def greet_width(o, carry):
        pl.semaphore_signal(
            barrier, inc=1, device_id={"expert": me, "width": lax.rem(mw + o, n_width)}, device_id_type=MESH
        )
        return carry

    def greet_beside(o, carry):
        for dy, dz in BESIDE:
            pl.semaphore_signal(
                barrier, inc=1, device_id={"expert": target(dy, dz), "width": lax.rem(mw + o, n_width)},
                device_id_type=MESH,
            )
        return carry

    lax.fori_loop(1, n, greet_expert, 0)
    lax.fori_loop(1, n_width, greet_width, 0)
    lax.fori_loop(1, n_width, greet_beside, 0)

    loads = [
        pltpu.make_async_copy(src, dst, in_sem.at[i])
        for i, (src, dst) in enumerate((
            (ids_hbm, ids_ref),
            (slots_hbm, slots_ref),
            (grad_hbm.at[:, pl.ds(0, c0)], x0.at[0]),
            (grad_hbm.at[:, pl.ds(c0, cols[1][1])], x1.at[0]),
            (tok_hbm, tok),
            (weight_hbm, weight),
            (eo_hbm, eo),
        ))
    ]
    for load in loads:
        load.start()
    loads[0].wait()
    loads[1].wait()

    row16 = lax.broadcasted_iota(I32, (n, t_rows), 0)
    slot_tbl = jnp.full((n, t_rows), -1, I32)
    eloc_tbl = jnp.full((n, t_rows), -1, I32)
    for k in range(top):
        ids = ids_ref[k : k + 1, :]
        dev = lax.shift_right_logical(ids, 4)
        hit = row16 == dev
        slot_tbl = jnp.where(hit, slots_ref[k : k + 1, :], slot_tbl)
        eloc_tbl = jnp.where(hit, ids - dev * PER_DEV, eloc_tbl)
    slot_own[...] = slot_tbl
    eloc[...] = eloc_tbl
    slot_f = slot_tbl.astype(F32)
    tbf0[0] = slot_f
    tbf1[0] = slot_f
    tb_own[...] = slot_f.astype(BF16)
    dsend[...] = jnp.zeros_like(dsend)

    pl.semaphore_wait(barrier, n - 1 + (1 + len(BESIDE)) * (n_width - 1))

    def first_copy(g, k):
        step, h = ((1, 0), (-1, 1), (1, 1), (-1, 0))[k]
        rows = pl.ds(h * t_half, t_half)
        return to(
            xs_of[g].at[0, rows], xs_of[g].at[step % SIDE, rows], xs.at[g], xr.at[g, min(k, 2)], e=ring1(g, step)
        )

    def onward_copy(g, k):
        step, h = ((1, 0), (-1, 1))[k]
        rows = pl.ds(h * t_half, t_half)
        return to(xs_of[g].at[step % SIDE, rows], xs_of[g].at[2, rows], xs.at[g], xr.at[g, 3], e=ring1(g, step))

    def table_copy(g, j):
        return to(tb_own, tb_in[g].at[j], tbs.at[g], tbr.at[g, j // 2 * (3 - j)], e=ring1(g, j))

    for g in range(2):
        loads[2 + g].wait()
        first_copy(g, 0).start()
        first_copy(g, 1).start()
    for g in range(2):
        for j in (1, 3, 2):
            table_copy(g, j).start()
    for g in range(2):
        first_copy(g, 2).start()
        first_copy(g, 3).start()

    loads[4].wait()
    loads[5].wait()
    logits_t = jnp.dot(tok[...], weight[...], preferred_element_type=F32).T
    for d in range(n):
        block = logits_t[d * PER_DEV : (d + 1) * PER_DEV, :]
        hit = row16[:PER_DEV] == eloc_tbl[d : d + 1, :]
        lsend[d : d + 1, :] = jnp.sum(jnp.where(hit, block, 0.0), axis=0, keepdims=True)

    slot_iota = lax.broadcasted_iota(I32, (ROW, t_rows), 0).astype(F32)

    def own_table(d, carry):
        row = tbf0[0, pl.ds(d, 1), :]
        oh[d] = jnp.where(row == slot_iota, 1.0, 0.0).astype(BF16)
        return carry

    lax.fori_loop(0, n, own_table, 0)
    win[mw] = lsend[...]

    def logit_copy(o):
        return to(lsend, win.at[mw], ws, wr, w=lax.rem(mw + o, n_width))

    def send_logits(o, carry):
        logit_copy(o).start()
        return carry

    lax.fori_loop(1, n_width, send_logits, 0)

    cap_iota = lax.broadcasted_iota(I32, (cap, t_rows), 0).astype(F32)

    def select(g, j0, step, count):
        def one(i, carry):
            j, m = j0 + step * (i // SIDE), lax.rem(i, SIDE)
            row = tbf[g][j, pl.ds(ring2(g, m), 1), :]
            pick = jnp.where(row == cap_iota, 1.0, 0.0).astype(BF16)
            rows = jnp.dot(pick, xs_of[g][j], preferred_element_type=F32).astype(BF16)
            away = (m + SIDE - 1) // SIDE
            home = place(g, p1[g] - j, p2[g])
            rs_of[g][home * (1 - away) + away * (n + j * SIDE + m)] = rows
            return carry

        lax.fori_loop(0, count * SIDE, one, 0)

    def near_copy(g, j, kind):
        step = (1, -1)[kind]
        return to(
            rs_of[g].at[n + j * SIDE + step % SIDE], rs_of[g].at[place(g, p1[g] - j, p2[g])],
            ss.at[g], sr.at[g, (0, 1, 2, 1)[j]], e=ring2(g, step),
        )

    def far_copy(g, j):
        return to(
            rs_of[g].at[n + j * SIDE + 2], rs_of[g].at[place(g, p1[g] - j, p2[g])],
            ss.at[g], sr.at[g, 3 + (0, 1, 2, 1)[j]], e=ring2(g, 2),
        )

    def send_far(j):
        for g in range(2):
            far_copy(g, j).start()

    def send_near(j):
        for g in range(2):
            near_copy(g, j, 0).start()
            near_copy(g, j, 1).start()

    def arrived(index, count):
        for g in range(2):
            await_recv(rs_of[g].at[pl.ds(0, count)], sr.at[g, index])

    for g in range(2):
        select(g, 0, 0, 1)
    for k in range(2):
        for g in range(2):
            await_recv(xs_of[g].at[0, pl.ds(0, t_half)], xr.at[g, k])
            onward_copy(g, k).start()
    send_far(0)

    await_recv(win.at[pl.ds(0, n_width - 1)], wr)
    total_logits = win[0]
    for w in range(1, win.shape[0]):
        total_logits = total_logits + win[w]
    picked = jnp.where(eloc_tbl >= 0, jax.nn.sigmoid(total_logits), 0.0)
    picked_v[...] = picked
    gates = (ROUTE_SCALE * picked / jnp.sum(picked, axis=0, keepdims=True)).astype(BF16).astype(F32)

    def gate_row(d, acc):
        only = jnp.where(row16 == d, gates, 0.0).astype(BF16)
        return acc + lax.dot_general(only, oh[d], NT, preferred_element_type=F32)

    gate_slots = lax.fori_loop(0, n, gate_row, jnp.zeros((n, ROW), F32))
    for d in range(n):
        gsend[d] = gate_slots[d : d + 1, :]
    gin[me] = gsend[me]

    def gate_copy(o):
        d = lax.rem(me + o, n)
        return to(gsend.at[d], gin.at[me], gs, gr, e=d)

    def send_gates(o, carry):
        gate_copy(o).start()
        return carry

    lax.fori_loop(1, n, send_gates, 0)

    def take_tables(js):
        for g in range(2):
            await_recv(tb_in[g].at[pl.ds(0, len(js))], tbr.at[g, len(js) % 2])
            for j in js:
                tbf[g][j] = tb_in[g][j].astype(F32)

    take_tables((1, 3))
    for g in range(2):
        await_recv(xs_of[g].at[0], xr.at[g, 2])
        select(g, 1, 2, 2)
    send_far(1)
    send_far(3)
    send_near(1)
    take_tables((2,))
    for g in range(2):
        await_recv(xs_of[g].at[0], xr.at[g, 3])
        select(g, 2, 0, 1)
    send_far(2)
    send_near(2)
    send_near(3)

    loads[6].wait()
    await_recv(gin.at[pl.ds(0, n - 1)], gr)

    ones = jnp.ones((8, 128), BF16)
    eye = lax.broadcasted_iota(I32, (cap, cap), 0) == lax.broadcasted_iota(I32, (cap, cap), 1)

    def gate_grads_of(s):
        acc = None
        for g in range(2):
            for at in range(0, cols[g][1], 128):
                a = rs_of[g][s, :, at : at + 128].astype(F32)
                b = eo[s, :, cols[g][0] + at : cols[g][0] + at + 128].astype(F32)
                acc = a * b if acc is None else acc + a * b
        high = acc.astype(BF16)
        low = (acc - high.astype(F32)).astype(BF16)
        dots = lax.dot_general(ones, high, NT, preferred_element_type=F32)
        dots = dots + lax.dot_general(ones, low, NT, preferred_element_type=F32)
        dsend[s, :, :cap] = dots[0:1, :]

    def expert_grad_of(s):
        scale = jnp.where(eye, gin[s][:, :cap], 0.0).astype(BF16)
        for g in range(2):
            value = jnp.dot(scale, rs_of[g][s], preferred_element_type=F32)
            egv[s, :, cols[g][0] : cols[g][0] + cols[g][1]] = value.astype(BF16)

    def far_one(i):
        return 2 * i, 2 - 2 * i

    def far_near(i):
        q, r = i // 2, 1 + 2 * lax.rem(i, 2)
        return 2 * q + (1 - q) * r, q * r + 2 * (1 - q)

    def diagonal(i):
        return 1 + 2 * (i // 2), 1 + 2 * lax.rem(i, 2)

    def beside(i):
        q, r = i // 2, 1 + 2 * lax.rem(i, 2)
        return q * r, (1 - q) * r

    def grads_back(count, offset, row, index):
        def one(i, carry):
            s = origin(*offset(i))
            gate_grads_of(s)
            to(dsend.at[s], rin.at[row + i], rts.at[0], rtr.at[index], e=s).start()
            return carry

        lax.fori_loop(0, count, one, 0)

    def scaled(count, offset):
        def one(i, carry):
            expert_grad_of(origin(*offset(i)))
            return carry

        lax.fori_loop(0, count, one, 0)

    def width_copy(o, start, count, index):
        rows = pl.ds(start, count)
        return to(rin.at[rows], win2.at[mw, rows], w2s.at[index], w2r.at[index], w=lax.rem(mw + o, n_width))

    def to_widths(start, count, index):
        def one(o, carry):
            width_copy(o, start, count, index).start()
            return carry

        lax.fori_loop(1, n_width, one, 0)
        rows = pl.ds(start, count)
        win2[mw, rows] = rin[rows]

    gate_grads_of(me)
    rin[0] = dsend[me]
    arrived(3, 1)
    grads_back(2, far_one, 1, 0)
    arrived(5, 1)
    grads_back(1, lambda i: (2, 2), 3, 0)
    scaled(1, lambda i: (0, 0))
    scaled(2, far_one)
    scaled(1, lambda i: (2, 2))
    arrived(2, 2)
    arrived(4, 2)
    grads_back(4, far_near, 4, 0)
    send_near(0)
    scaled(4, far_near)
    arrived(1, 4)
    grads_back(4, diagonal, EARLY, 1)
    scaled(4, diagonal)
    await_recv(dsend.at[pl.ds(0, EARLY - 1)], rtr.at[0])
    to_widths(0, EARLY, 0)
    arrived(0, 2)

    def late_grads(i, carry):
        gate_grads_of(origin(*beside(i)))
        return carry

    def late_copy(i, w):
        s = origin(*beside(i))
        return to(dsend.at[s], win2.at[mw, EARLY + MIDDLE + i], rts.at[1], w2r.at[2], e=s, w=w)

    def late_send(i, carry):
        def one(w, inner):
            late_copy(i, w).start()
            return inner

        return lax.fori_loop(0, n_width, one, carry)

    lax.fori_loop(0, LATE, late_grads, 0)
    lax.fori_loop(0, LATE, late_send, 0)
    await_recv(dsend.at[pl.ds(0, MIDDLE)], rtr.at[1])
    to_widths(EARLY, MIDDLE, 1)
    scaled(4, beside)

    await_recv(win2.at[pl.ds(0, n_width - 1), pl.ds(0, EARLY)], w2r.at[0])
    await_recv(win2.at[pl.ds(0, n_width - 1), pl.ds(0, MIDDLE)], w2r.at[1])
    await_recv(win2.at[pl.ds(0, n_width), pl.ds(0, LATE)], w2r.at[2])
    for i, (dy, dz) in enumerate(OFFSETS):
        row = win2[0, i]
        for w in range(1, win2.shape[0]):
            row = row + win2[w, i]
        ggv[pl.ds(target(dy, dz), 1), :] = row

    slots = slot_own[...]
    lane = jnp.bitwise_and(slots, 127)
    pieces = []
    for at in range(0, t_rows, 128):
        index = lane[:, at : at + 128]
        low = jnp.take_along_axis(ggv[:, 0:128], index, axis=1)
        high = jnp.take_along_axis(ggv[:, 128:256], index, axis=1)
        pieces.append(jnp.where(slots[:, at : at + 128] < 128, low, high))
    chosen = slots >= 0
    gate_grads = jnp.where(chosen, jnp.concatenate(pieces, axis=1), 0.0)

    picked = picked_v[...]
    totals = jnp.sum(picked, axis=0, keepdims=True)
    weighted = jnp.sum(gate_grads * picked, axis=0, keepdims=True) / totals
    local = jnp.where(chosen, ROUTE_SCALE / totals * (gate_grads - weighted) * picked * (1.0 - picked), 0.0)
    for d in range(n):
        hit = row16[:PER_DEV] == eloc[d : d + 1, :]
        block = jnp.where(hit, local[d : d + 1, :], 0.0)
        lgt32[d * PER_DEV : (d + 1) * PER_DEV, :] = block
        lgt[d * PER_DEV : (d + 1) * PER_DEV, :] = block.astype(BF16)

    part = jnp.dot(lgt[...], tok[...], preferred_element_type=F32)
    rb[...] = part.astype(BF16).reshape(rb.shape)

    logit_grads = lgt32[...].T.astype(BF16)
    for dy, dz in FAR_BOTH + FAR_NEAR + FAR_ONE + DIAGONAL + BESIDE:
        d = target(dy, dz)
        to(rb.at[d], rr.at[me], rps, rpr, e=d).start()
    rr[me] = rb[me]
    ig_ref[...] = lax.dot_general(logit_grads, weight[...], NT, preferred_element_type=F32).astype(BF16)
    await_recv(rb.at[pl.ds(0, n - 1)], rpr)
    total = rr[0].astype(F32)
    for d in range(1, n):
        total = total + rr[d].astype(F32)
    rg_ref[...] = total

    for g in range(2):
        await_sent(xs_of[g].at[pl.ds(0, SIDE - 1)], xs.at[g])
        await_sent(tb_in[g].at[pl.ds(0, SIDE - 1)], tbs.at[g])
        await_sent(rs_of[g].at[pl.ds(0, (SIDE - 1) * SIDE)], ss.at[g])
    await_sent(win.at[pl.ds(0, n_width - 1)], ws)
    await_sent(gin.at[pl.ds(0, n - 1)], gs)
    await_sent(dsend.at[pl.ds(0, EARLY + MIDDLE - 1)], rts.at[0])
    await_sent(win2.at[pl.ds(0, n_width), pl.ds(0, LATE)], rts.at[1])
    await_sent(win2.at[pl.ds(0, n_width - 1), pl.ds(0, EARLY)], w2s.at[0])
    await_sent(win2.at[pl.ds(0, n_width - 1), pl.ds(0, MIDDLE)], w2s.at[1])
    await_sent(rb.at[pl.ds(0, n - 1)], rps)


def write_out(eg_in, rg_in, ig_in, eg_out, rg_out, ig_out, sem):
    copies = [
        pltpu.make_async_copy(src, dst, sem.at[i])
        for i, (src, dst) in enumerate(((eg_in, eg_out), (ig_in, ig_out), (rg_in, rg_out)))
    ]
    for copy in copies:
        copy.start()
    for copy in copies:
        copy.wait()


def body(tokens_in, out_grad, router_weight, expert_out, expert_ids, slot_ids):
    n = lax.axis_size("expert")
    n_width = lax.axis_size("width")
    t_rows, d_cols = out_grad.shape
    top = expert_ids.shape[1]
    experts = router_weight.shape[1]
    cap = t_rows * top // n
    c0 = (d_cols // 128 + 1) // 2 * 128
    c1 = d_cols - c0
    hbm, vmem = pl.BlockSpec(memory_space=pltpu.HBM), pl.BlockSpec(memory_space=pltpu.VMEM)
    dma = pltpu.SemaphoreType.DMA
    scratch = [
        pltpu.VMEM((SIDE, t_rows, c0), BF16),
        pltpu.VMEM((SIDE, t_rows, c1), BF16),
        pltpu.VMEM((2 * n, cap, c0), BF16),
        pltpu.VMEM((2 * n, cap, c1), BF16),
        pltpu.VMEM((t_rows, d_cols), BF16),
        pltpu.VMEM((d_cols, experts), BF16),
        pltpu.VMEM((n, cap, d_cols), BF16),
        pltpu.VMEM((top, t_rows), I32),
        pltpu.VMEM((top, t_rows), I32),
        pltpu.VMEM((n, ROW, t_rows), BF16),
        pltpu.VMEM((n, t_rows), BF16),
        pltpu.VMEM((SIDE, n, t_rows), BF16),
        pltpu.VMEM((SIDE, n, t_rows), BF16),
        pltpu.VMEM((SIDE, n, t_rows), F32),
        pltpu.VMEM((SIDE, n, t_rows), F32),
        pltpu.VMEM((n, t_rows), I32),
        pltpu.VMEM((n, t_rows), I32),
        pltpu.VMEM((n, t_rows), F32),
        pltpu.VMEM((n_width, n, t_rows), F32),
        pltpu.VMEM((n, 1, ROW), F32),
        pltpu.VMEM((n, 1, ROW), F32),
        pltpu.VMEM((n, 1, ROW), F32),
        pltpu.VMEM((EARLY + MIDDLE, 1, ROW), F32),
        pltpu.VMEM((n_width, n, 1, ROW), F32),
        pltpu.VMEM((n, ROW), F32),
        pltpu.VMEM((n, t_rows), F32),
        pltpu.VMEM((experts, t_rows), F32),
        pltpu.VMEM((experts, t_rows), BF16),
        pltpu.VMEM((n, experts // n, d_cols), BF16),
        pltpu.VMEM((n, experts // n, d_cols), BF16),
        dma((7,)),
        dma((2,)), dma((2, 4)),
        dma((2,)), dma((2, 2)),
        dma(()), dma(()),
        dma(()), dma(()),
        dma((2,)), dma((2, 6)),
        dma((2,)), dma((2,)),
        dma((2,)), dma((3,)),
        dma(()), dma(()),
    ]
    expert_grad, router_grad, input_grad = pl.pallas_call(
        kernel,
        out_shape=(
            pltpu.VMEM((n, cap, d_cols), BF16),
            pltpu.VMEM((experts // n, d_cols), F32),
            pltpu.VMEM((t_rows, d_cols), BF16),
        ),
        in_specs=[hbm] * 6,
        out_specs=(vmem, vmem, vmem),
        scratch_shapes=scratch,
        compiler_params=pltpu.CompilerParams(
            collective_id=0, has_side_effects=True, vmem_limit_bytes=46 * 1024 * 1024
        ),
    )(*(
        pltpu.with_memory_space_constraint(a, pltpu.HBM)
        for a in (tokens_in, out_grad, router_weight, expert_out.reshape(n, cap, d_cols), expert_ids.T, slot_ids.T)
    ))
    expert_grad, router_grad, input_grad = pl.pallas_call(
        write_out,
        out_shape=(
            jax.ShapeDtypeStruct((n, cap, d_cols), BF16),
            jax.ShapeDtypeStruct((experts // n, d_cols), F32),
            jax.ShapeDtypeStruct((t_rows, d_cols), BF16),
        ),
        in_specs=[vmem, vmem, vmem],
        out_specs=(hbm, hbm, hbm),
        scratch_shapes=[dma((3,))],
        compiler_params=pltpu.CompilerParams(vmem_limit_bytes=2 * 1024 * 1024),
    )(*(pltpu.with_memory_space_constraint(a, pltpu.VMEM) for a in (expert_grad, router_grad, input_grad)))
    return expert_grad.reshape(n * cap, d_cols), router_grad.T, input_grad


def solution(mesh):
    return jax.shard_map(
        body,
        mesh=mesh,
        in_specs=(
            P("expert", "width"),
            P("expert", "width"),
            P("width", None),
            P("expert", "width"),
            P("expert", None),
            P("expert", None),
        ),
        out_specs=(P("expert", "width"), P("width", "expert"), P("expert", "width")),
        check_vma=False,
    )
```

time: 81.3 us -> 70.8 us (0.87)
  local copies, waits for them, and re-layouts: 6.99 us -> 0 us
  Pallas kernels: 73.4 us -> 69.7 us
    unnamed x7 -> x0, local copies, waits for them, and re-layouts: 6.99 us -> none
    pallas_call x1 -> x2, Pallas kernels: 73.4 us -> 69.7 us  [the longest x1 67 us: body(): pl.pallas_call(kernel, out_shape=(pltpu.VMEM((n, cap, d_cols), BF16), plt...]
where the time goes in v2:
time: 70.8 us; the launch traced here: 70.3 us
  Pallas kernels  69.7 us (98%)
    pallas_call x1, Pallas kernels, body(): pl.pallas_call(kernel, out_shape=(pltpu.VMEM((n, cap, d_cols), BF16), plt...  67 us
    pallas_call x1, Pallas kernels, body(): pl.pallas_call(write_out, out_shape=(jax.ShapeDtypeStruct((n, cap, d_cols...  2.69 us

profile of v2, /device:TPU:0, one launch (start us, length us, event | category | flops | bytes accessed | tf_op | source)
XLA Modules:
  0.0 70.3 jit_solution(9288085509327270358)
XLA Ops:
  0.6 67.0 %shard_map.85 = (bf16[16,192,896]{2,1,0:T(8,128)(2,1)S(1)}, f32[16,896]{1,0:T(8,128)S(1)}, bf16[384,896]{1,0:T(8,128)(2,1)S(1)}) custom-call(bf16[384,896]{1,0:T(8,128)(2,1)} %tok_hbm.1, bf16[384,896]{1,0:T(8,128)(2,1)} %grad_hbm.1, bf16[896,256]{1,0:T(8,128)(2,1)} %weight_hbm.1, bf16[16,192,896]{2,1,0:T(8,128)(2,1)} %bitcast.5, s32[8,384]{1,0:T(8,128)} %bitcast.6, ...), custom_call_target="tpu_custom_call" | custom-call | tf_op jit(solution)/shard_map/pallas_call | solution.py:528
  67.7 2.7 %shard_map.86 = (bf16[16,192,896]{2,1,0:T(8,128)(2,1)}, f32[16,896]{1,0:T(8,128)}, bf16[384,896]{1,0:T(8,128)(2,1)}) custom-call(bf16[16,192,896]{2,1,0:T(8,128)(2,1)S(1)} %get-tuple-element.9.eg_in, f32[16,896]{1,0:T(8,128)S(1)} %get-tuple-element.10.rg_in, bf16[384,896]{1,0:T(8,128)(2,1)S(1)} %get-tuple-element.11.ig_in), custom_call_target="tpu_custom_call" | custom-call | tf_op jit(solution)/shard_map/pallas_call | solution.py:545

commit v3 on v2

--- a/solution.py
+++ b/solution.py
@@ -22,17 +22,19 @@
 FAR_NEAR = ((1, 2), (3, 2), (2, 1), (2, 3))
 DIAGONAL = ((1, 1), (1, 3), (3, 1), (3, 3))
 BESIDE = ((0, 1), (0, 3), (1, 0), (3, 0))
-OFFSETS = SELF + FAR_ONE + FAR_BOTH + FAR_NEAR + DIAGONAL + BESIDE
-EARLY, MIDDLE, LATE = 8, 4, 4
+OFFSETS = SELF + FAR_ONE + FAR_NEAR + FAR_BOTH + DIAGONAL + BESIDE
+LATE_ONES = DIAGONAL + BESIDE
+EARLY, LATE = 8, 8
+ROUNDS = 4
 
 
 def kernel(
     tok_hbm, grad_hbm, weight_hbm, eo_hbm, ids_hbm, slots_hbm,
     egv, rg_ref, ig_ref,
-    x0, x1, rs0, rs1, tok, weight, eo, ids_ref, slots_ref, oh,
+    x0, x1, rs0, rs1, rl0, rl1, tok, weight, eo, ids_ref, slots_ref, oh,
     tb_own, tb_in0, tb_in1, tbf0, tbf1, slot_own, eloc, lsend, win, gsend, gin, dsend, rin, win2,
     ggv, picked_v, lgt32, lgt, rb, rr,
-    in_sem, xs, xr, tbs, tbr, ws, wr, gs, gr, ss, sr, rts, rtr, w2s, w2r, rps, rpr,
+    known, in_sem, xs, xr, tbs, tbr, ws, wr, gs, gr, ss, sr, rls, rlr, rts, rtr, w2s, w2r, rps, rpr,
 ):
     n = lax.axis_size("expert")
     n_width = lax.axis_size("width")
@@ -41,7 +43,8 @@
     top, t_rows = ids_ref.shape
     cap = rs0.shape[1]
     t_half = t_rows // 2
-    xs_of, rs_of = (x0, x1), (rs0, rs1)
+    half = cap // 2
+    xs_of, rs_of, rl_of = (x0, x1), (rs0, rs1), (rl0, rl1)
     tb_in, tbf = (tb_in0, tb_in1), (tbf0, tbf1)
     c0 = x0.shape[2]
     cols = ((0, c0), (c0, x1.shape[2]))
@@ -84,37 +87,33 @@
 
     barrier = pltpu.get_barrier_semaphore()
 
-    def greet_expert(o, carry):
+    x_here = mw // 2
+    xs_count = n_width // 2
+
+    def greet(sem):
+        for dy, dz in BESIDE:
+            pl.semaphore_signal(sem, inc=1, device_id={"expert": target(dy, dz), "width": mw}, device_id_type=MESH)
+        for step in (1, xs_count - 1):
+            w = lax.rem(x_here + step, xs_count) * 2 + core
+            pl.semaphore_signal(sem, inc=1, device_id={"expert": me, "width": w}, device_id_type=MESH)
         pl.semaphore_signal(
-            barrier, inc=1, device_id={"expert": lax.rem(me + o, n), "width": mw}, device_id_type=MESH
+            sem, inc=1, device_id={"expert": me, "width": x_here * 2 + 1 - core}, device_id_type=MESH
         )
-        return carry
-
-    def greet_width(o, carry):
-        pl.semaphore_signal(
-            barrier, inc=1, device_id={"expert": me, "width": lax.rem(mw + o, n_width)}, device_id_type=MESH
-        )
-        return carry
-
-    def greet_beside(o, carry):
-        for dy, dz in BESIDE:
-            pl.semaphore_signal(
-                barrier, inc=1, device_id={"expert": target(dy, dz), "width": lax.rem(mw + o, n_width)},
-                device_id_type=MESH,
-            )
-        return carry
-
-    lax.fori_loop(1, n, greet_expert, 0)
-    lax.fori_loop(1, n_width, greet_width, 0)
-    lax.fori_loop(1, n_width, greet_beside, 0)
+
+    def take_round(k):
+        pl.semaphore_wait(known.at[k], len(BESIDE) + 3)
+        if k + 1 < ROUNDS:
+            greet(known.at[k + 1])
+
+    greet(barrier)
 
     loads = [
         pltpu.make_async_copy(src, dst, in_sem.at[i])
         for i, (src, dst) in enumerate((
+            (grad_hbm.at[:, pl.ds(0, c0)], x0.at[0]),
+            (grad_hbm.at[:, pl.ds(c0, cols[1][1])], x1.at[0]),
             (ids_hbm, ids_ref),
             (slots_hbm, slots_ref),
-            (grad_hbm.at[:, pl.ds(0, c0)], x0.at[0]),
-            (grad_hbm.at[:, pl.ds(c0, cols[1][1])], x1.at[0]),
             (tok_hbm, tok),
             (weight_hbm, weight),
             (eo_hbm, eo),
@@ -122,9 +121,31 @@
     ]
     for load in loads:
         load.start()
-    loads[0].wait()
-    loads[1].wait()
-
+
+    pl.semaphore_wait(barrier, len(BESIDE) + 3)
+
+    def first_copy(g, k):
+        step, h = ((1, 0), (-1, 1), (1, 1), (-1, 0))[k]
+        rows = pl.ds(h * t_half, t_half)
+        return to(
+            xs_of[g].at[0, rows], xs_of[g].at[step % SIDE, rows], xs.at[g], xr.at[g, min(k, 2)], e=ring1(g, step)
+        )
+
+    def onward_copy(g, k):
+        step, h = ((1, 0), (-1, 1))[k]
+        rows = pl.ds(h * t_half, t_half)
+        return to(xs_of[g].at[step % SIDE, rows], xs_of[g].at[2, rows], xs.at[g], xr.at[g, 3], e=ring1(g, step))
+
+    def table_copy(g, j):
+        return to(tb_own, tb_in[g].at[j], tbs.at[g], tbr.at[g, j // 2 * (3 - j)], e=ring1(g, j))
+
+    for g in range(2):
+        loads[g].wait()
+        first_copy(g, 0).start()
+        first_copy(g, 1).start()
+    greet(known.at[0])
+    loads[2].wait()
+    loads[3].wait()
     row16 = lax.broadcasted_iota(I32, (n, t_rows), 0)
     slot_tbl = jnp.full((n, t_rows), -1, I32)
     eloc_tbl = jnp.full((n, t_rows), -1, I32)
@@ -142,30 +163,9 @@
     tb_own[...] = slot_f.astype(BF16)
     dsend[...] = jnp.zeros_like(dsend)
 
-    pl.semaphore_wait(barrier, n - 1 + (1 + len(BESIDE)) * (n_width - 1))
-
-    def first_copy(g, k):
-        step, h = ((1, 0), (-1, 1), (1, 1), (-1, 0))[k]
-        rows = pl.ds(h * t_half, t_half)
-        return to(
-            xs_of[g].at[0, rows], xs_of[g].at[step % SIDE, rows], xs.at[g], xr.at[g, min(k, 2)], e=ring1(g, step)
-        )
-
-    def onward_copy(g, k):
-        step, h = ((1, 0), (-1, 1))[k]
-        rows = pl.ds(h * t_half, t_half)
-        return to(xs_of[g].at[step % SIDE, rows], xs_of[g].at[2, rows], xs.at[g], xr.at[g, 3], e=ring1(g, step))
-
-    def table_copy(g, j):
-        return to(tb_own, tb_in[g].at[j], tbs.at[g], tbr.at[g, j // 2 * (3 - j)], e=ring1(g, j))
-
-    for g in range(2):
-        loads[2 + g].wait()
-        first_copy(g, 0).start()
-        first_copy(g, 1).start()
-    for g in range(2):
-        for j in (1, 3, 2):
-            table_copy(g, j).start()
+    for g in range(2):
+        table_copy(g, 1).start()
+        table_copy(g, 3).start()
     for g in range(2):
         first_copy(g, 2).start()
         first_copy(g, 3).start()
@@ -178,6 +178,10 @@
         hit = row16[:PER_DEV] == eloc_tbl[d : d + 1, :]
         lsend[d : d + 1, :] = jnp.sum(jnp.where(hit, block, 0.0), axis=0, keepdims=True)
 
+    take_round(0)
+    for g in range(2):
+        table_copy(g, 2).start()
+
     slot_iota = lax.broadcasted_iota(I32, (ROW, t_rows), 0).astype(F32)
 
     def own_table(d, carry):
@@ -188,6 +192,8 @@
     lax.fori_loop(0, n, own_table, 0)
     win[mw] = lsend[...]
 
+    take_round(1)
+
     def logit_copy(o):
         return to(lsend, win.at[mw], ws, wr, w=lax.rem(mw + o, n_width))
 
@@ -201,38 +207,58 @@
 
     def select(g, j0, step, count):
         def one(i, carry):
-            j, m = j0 + step * (i // SIDE), lax.rem(i, SIDE)
-            row = tbf[g][j, pl.ds(ring2(g, m), 1), :]
-            pick = jnp.where(row == cap_iota, 1.0, 0.0).astype(BF16)
-            rows = jnp.dot(pick, xs_of[g][j], preferred_element_type=F32).astype(BF16)
-            away = (m + SIDE - 1) // SIDE
-            home = place(g, p1[g] - j, p2[g])
-            rs_of[g][home * (1 - away) + away * (n + j * SIDE + m)] = rows
+            j = j0 + step * i
+            picks = []
+            for m in range(SIDE):
+                row = tbf[g][j, pl.ds(ring2(g, m), 1), :]
+                picks.append(jnp.where(row == cap_iota, 1.0, 0.0).astype(BF16))
+            rows = jnp.dot(jnp.concatenate(picks, axis=0), xs_of[g][j], preferred_element_type=F32).astype(BF16)
+            rs_of[g][place(g, p1[g] - j, p2[g])] = rows[:cap]
+            for m in range(1, SIDE):
+                rs_of[g][n + j * SIDE + m] = rows[m * cap : (m + 1) * cap]
             return carry
 
-        lax.fori_loop(0, count * SIDE, one, 0)
-
-    def near_copy(g, j, kind):
+        if count == 1:
+            one(0, 0)
+        else:
+            lax.fori_loop(0, count, one, 0)
+
+    def near_copy(g, j, kind, start, rows):
         step = (1, -1)[kind]
+        rows = pl.ds(start, rows)
         return to(
-            rs_of[g].at[n + j * SIDE + step % SIDE], rs_of[g].at[place(g, p1[g] - j, p2[g])],
+            rs_of[g].at[n + j * SIDE + step % SIDE, rows], rs_of[g].at[place(g, p1[g] - j, p2[g]), rows],
             ss.at[g], sr.at[g, (0, 1, 2, 1)[j]], e=ring2(g, step),
         )
 
-    def far_copy(g, j):
+    def relay_copy(g, j, h):
         return to(
-            rs_of[g].at[n + j * SIDE + 2], rs_of[g].at[place(g, p1[g] - j, p2[g])],
-            ss.at[g], sr.at[g, 3 + (0, 1, 2, 1)[j]], e=ring2(g, 2),
+            rs_of[g].at[n + j * SIDE + 2, pl.ds(h * half, half)], rl_of[g].at[j, h],
+            ss.at[g], rlr.at[g, j], e=ring2(g, (1, -1)[h]),
+        )
+
+    def final_copy(g, j, h):
+        step = (1, -1)[h]
+        return to(
+            rl_of[g].at[j, h], rs_of[g].at[place(g, p1[g] - j, p2[g] - step), pl.ds(h * half, half)],
+            rls.at[g], sr.at[g, 3 + (0, 1, 2, 1)[j]], e=ring2(g, step),
         )
 
     def send_far(j):
         for g in range(2):
-            far_copy(g, j).start()
-
-    def send_near(j):
+            relay_copy(g, j, 0).start()
+            relay_copy(g, j, 1).start()
+
+    def pass_on(j):
         for g in range(2):
-            near_copy(g, j, 0).start()
-            near_copy(g, j, 1).start()
+            await_recv(rl_of[g].at[j], rlr.at[g, j])
+            final_copy(g, j, 0).start()
+            final_copy(g, j, 1).start()
+
+    def send_near(j, start=0, rows=cap):
+        for g in range(2):
+            near_copy(g, j, 0, start, rows).start()
+            near_copy(g, j, 1, start, rows).start()
 
     def arrived(index, count):
         for g in range(2):
@@ -245,6 +271,7 @@
             await_recv(xs_of[g].at[0, pl.ds(0, t_half)], xr.at[g, k])
             onward_copy(g, k).start()
     send_far(0)
+    send_near(0, 0, half)
 
     await_recv(win.at[pl.ds(0, n_width - 1)], wr)
     total_logits = win[0]
@@ -263,6 +290,8 @@
         gsend[d] = gate_slots[d : d + 1, :]
     gin[me] = gsend[me]
 
+    take_round(2)
+
     def gate_copy(o):
         d = lax.rem(me + o, n)
         return to(gsend.at[d], gin.at[me], gs, gr, e=d)
@@ -282,36 +311,42 @@
     take_tables((1, 3))
     for g in range(2):
         await_recv(xs_of[g].at[0], xr.at[g, 2])
+    for g in range(2):
         select(g, 1, 2, 2)
     send_far(1)
     send_far(3)
-    send_near(1)
+    pass_on(0)
     take_tables((2,))
     for g in range(2):
         await_recv(xs_of[g].at[0], xr.at[g, 3])
+    for g in range(2):
         select(g, 2, 0, 1)
     send_far(2)
+    pass_on(1)
+    pass_on(3)
     send_near(2)
-    send_near(3)
 
     loads[6].wait()
     await_recv(gin.at[pl.ds(0, n - 1)], gr)
 
-    ones = jnp.ones((8, 128), BF16)
+    ones = jnp.ones((8, 256), BF16)
     eye = lax.broadcasted_iota(I32, (cap, cap), 0) == lax.broadcasted_iota(I32, (cap, cap), 1)
 
-    def gate_grads_of(s):
-        acc = None
-        for g in range(2):
-            for at in range(0, cols[g][1], 128):
-                a = rs_of[g][s, :, at : at + 128].astype(F32)
-                b = eo[s, :, cols[g][0] + at : cols[g][0] + at + 128].astype(F32)
-                acc = a * b if acc is None else acc + a * b
-        high = acc.astype(BF16)
-        low = (acc - high.astype(F32)).astype(BF16)
-        dots = lax.dot_general(ones, high, NT, preferred_element_type=F32)
-        dots = dots + lax.dot_general(ones, low, NT, preferred_element_type=F32)
-        dsend[s, :, :cap] = dots[0:1, :]
+    def gate_grads_of(blocks):
+        found = []
+        for s in blocks:
+            acc = None
+            for g in range(2):
+                for at in range(0, cols[g][1], 128):
+                    a = rs_of[g][s, :, at : at + 128].astype(F32)
+                    b = eo[s, :, cols[g][0] + at : cols[g][0] + at + 128].astype(F32)
+                    acc = a * b if acc is None else acc + a * b
+            high = acc.astype(BF16)
+            low = (acc - high.astype(F32)).astype(BF16)
+            both = jnp.concatenate([high, low], axis=1)
+            found.append(lax.dot_general(ones, both, NT, preferred_element_type=F32)[0:1, :])
+        for s, dots in zip(blocks, found):
+            dsend[s, :, :cap] = dots
 
     def expert_grad_of(s):
         scale = jnp.where(eye, gin[s][:, :cap], 0.0).astype(BF16)
@@ -333,14 +368,25 @@
         q, r = i // 2, 1 + 2 * lax.rem(i, 2)
         return q * r, (1 - q) * r
 
-    def grads_back(count, offset, row, index):
-        def one(i, carry):
-            s = origin(*offset(i))
-            gate_grads_of(s)
-            to(dsend.at[s], rin.at[row + i], rts.at[0], rtr.at[index], e=s).start()
+    def grads_back(offsets, row):
+        blocks = [origin(dy, dz) for dy, dz in offsets]
+        gate_grads_of(blocks)
+        for i, s in enumerate(blocks):
+            to(dsend.at[s], rin.at[row + i], rts.at[0], rtr, e=s).start()
+
+    def late_copy(s, row, w):
+        return to(dsend.at[s], win2.at[mw, row], rts.at[1], w2r.at[1], e=s, w=w)
+
+    def grads_to_widths(offsets, row):
+        blocks = [origin(dy, dz) for dy, dz in offsets]
+        gate_grads_of(blocks)
+
+        def one(w, carry):
+            for i, s in enumerate(blocks):
+                late_copy(s, row + i, w).start()
             return carry
 
-        lax.fori_loop(0, count, one, 0)
+        lax.fori_loop(0, n_width, one, 0)
 
     def scaled(count, offset):
         def one(i, carry):
@@ -349,64 +395,45 @@
 
         lax.fori_loop(0, count, one, 0)
 
-    def width_copy(o, start, count, index):
-        rows = pl.ds(start, count)
-        return to(rin.at[rows], win2.at[mw, rows], w2s.at[index], w2r.at[index], w=lax.rem(mw + o, n_width))
-
-    def to_widths(start, count, index):
-        def one(o, carry):
-            width_copy(o, start, count, index).start()
-            return carry
-
-        lax.fori_loop(1, n_width, one, 0)
-        rows = pl.ds(start, count)
-        win2[mw, rows] = rin[rows]
-
-    gate_grads_of(me)
+    rows = pl.ds(0, EARLY)
+
+    def width_copy(o):
+        return to(rin, win2.at[mw, rows], w2s, w2r.at[0], w=lax.rem(mw + o, n_width))
+
+    def send_width(o, carry):
+        width_copy(o).start()
+        return carry
+
+    gate_grads_of([me])
     rin[0] = dsend[me]
     arrived(3, 1)
-    grads_back(2, far_one, 1, 0)
-    arrived(5, 1)
-    grads_back(1, lambda i: (2, 2), 3, 0)
+    grads_back(FAR_ONE, 1)
+    pass_on(2)
+    send_near(1)
     scaled(1, lambda i: (0, 0))
     scaled(2, far_one)
+    arrived(4, 2)
+    arrived(2, 2)
+    grads_back(FAR_NEAR, 3)
+    arrived(5, 1)
+    grads_back(FAR_BOTH, 7)
+    send_near(3)
+    send_near(0, half, half)
+    take_round(3)
+    scaled(4, far_near)
     scaled(1, lambda i: (2, 2))
-    arrived(2, 2)
-    arrived(4, 2)
-    grads_back(4, far_near, 4, 0)
-    send_near(0)
-    scaled(4, far_near)
+    await_recv(dsend.at[pl.ds(0, EARLY - 1)], rtr)
+    lax.fori_loop(1, n_width, send_width, 0)
+    win2[mw, rows] = rin[...]
     arrived(1, 4)
-    grads_back(4, diagonal, EARLY, 1)
+    grads_to_widths(DIAGONAL, EARLY)
+    arrived(0, 2)
+    grads_to_widths(BESIDE, EARLY + len(DIAGONAL))
     scaled(4, diagonal)
-    await_recv(dsend.at[pl.ds(0, EARLY - 1)], rtr.at[0])
-    to_widths(0, EARLY, 0)
-    arrived(0, 2)
-
-    def late_grads(i, carry):
-        gate_grads_of(origin(*beside(i)))
-        return carry
-
-    def late_copy(i, w):
-        s = origin(*beside(i))
-        return to(dsend.at[s], win2.at[mw, EARLY + MIDDLE + i], rts.at[1], w2r.at[2], e=s, w=w)
-
-    def late_send(i, carry):
-        def one(w, inner):
-            late_copy(i, w).start()
-            return inner
-
-        return lax.fori_loop(0, n_width, one, carry)
-
-    lax.fori_loop(0, LATE, late_grads, 0)
-    lax.fori_loop(0, LATE, late_send, 0)
-    await_recv(dsend.at[pl.ds(0, MIDDLE)], rtr.at[1])
-    to_widths(EARLY, MIDDLE, 1)
     scaled(4, beside)
 
     await_recv(win2.at[pl.ds(0, n_width - 1), pl.ds(0, EARLY)], w2r.at[0])
-    await_recv(win2.at[pl.ds(0, n_width - 1), pl.ds(0, MIDDLE)], w2r.at[1])
-    await_recv(win2.at[pl.ds(0, n_width), pl.ds(0, LATE)], w2r.at[2])
+    await_recv(win2.at[pl.ds(0, n_width), pl.ds(0, LATE)], w2r.at[1])
     for i, (dy, dz) in enumerate(OFFSETS):
         row = win2[0, i]
         for w in range(1, win2.shape[0]):
@@ -453,20 +480,21 @@
         await_sent(xs_of[g].at[pl.ds(0, SIDE - 1)], xs.at[g])
         await_sent(tb_in[g].at[pl.ds(0, SIDE - 1)], tbs.at[g])
         await_sent(rs_of[g].at[pl.ds(0, (SIDE - 1) * SIDE)], ss.at[g])
+        await_sent(rl_of[g], rls.at[g])
     await_sent(win.at[pl.ds(0, n_width - 1)], ws)
     await_sent(gin.at[pl.ds(0, n - 1)], gs)
-    await_sent(dsend.at[pl.ds(0, EARLY + MIDDLE - 1)], rts.at[0])
+    await_sent(dsend.at[pl.ds(0, EARLY - 1)], rts.at[0])
     await_sent(win2.at[pl.ds(0, n_width), pl.ds(0, LATE)], rts.at[1])
-    await_sent(win2.at[pl.ds(0, n_width - 1), pl.ds(0, EARLY)], w2s.at[0])
-    await_sent(win2.at[pl.ds(0, n_width - 1), pl.ds(0, MIDDLE)], w2s.at[1])
+    await_sent(win2.at[pl.ds(0, n_width - 1), pl.ds(0, EARLY)], w2s)
     await_sent(rb.at[pl.ds(0, n - 1)], rps)
 
 
 def write_out(eg_in, rg_in, ig_in, eg_out, rg_out, ig_out, sem):
-    copies = [
-        pltpu.make_async_copy(src, dst, sem.at[i])
-        for i, (src, dst) in enumerate(((eg_in, eg_out), (ig_in, ig_out), (rg_in, rg_out)))
-    ]
+    pieces = 4
+    step = eg_in.shape[0] // pieces
+    pairs = [(eg_in.at[pl.ds(i * step, step)], eg_out.at[pl.ds(i * step, step)]) for i in range(pieces)]
+    pairs += [(ig_in, ig_out), (rg_in, rg_out)]
+    copies = [pltpu.make_async_copy(src, dst, sem.at[i]) for i, (src, dst) in enumerate(pairs)]
     for copy in copies:
         copy.start()
     for copy in copies:
@@ -489,6 +517,8 @@
         pltpu.VMEM((SIDE, t_rows, c1), BF16),
         pltpu.VMEM((2 * n, cap, c0), BF16),
         pltpu.VMEM((2 * n, cap, c1), BF16),
+        pltpu.VMEM((SIDE, 2, cap // 2, c0), BF16),
+        pltpu.VMEM((SIDE, 2, cap // 2, c1), BF16),
         pltpu.VMEM((t_rows, d_cols), BF16),
         pltpu.VMEM((d_cols, experts), BF16),
         pltpu.VMEM((n, cap, d_cols), BF16),
@@ -507,7 +537,7 @@
         pltpu.VMEM((n, 1, ROW), F32),
         pltpu.VMEM((n, 1, ROW), F32),
         pltpu.VMEM((n, 1, ROW), F32),
-        pltpu.VMEM((EARLY + MIDDLE, 1, ROW), F32),
+        pltpu.VMEM((EARLY, 1, ROW), F32),
         pltpu.VMEM((n_width, n, 1, ROW), F32),
         pltpu.VMEM((n, ROW), F32),
         pltpu.VMEM((n, t_rows), F32),
@@ -515,14 +545,16 @@
         pltpu.VMEM((experts, t_rows), BF16),
         pltpu.VMEM((n, experts // n, d_cols), BF16),
         pltpu.VMEM((n, experts // n, d_cols), BF16),
+        pltpu.SemaphoreType.REGULAR((ROUNDS,)),
         dma((7,)),
         dma((2,)), dma((2, 4)),
         dma((2,)), dma((2, 2)),
         dma(()), dma(()),
         dma(()), dma(()),
         dma((2,)), dma((2, 6)),
-        dma((2,)), dma((2,)),
-        dma((2,)), dma((3,)),
+        dma((2,)), dma((2, SIDE)),
+        dma((2,)), dma(()),
+        dma(()), dma((2,)),
         dma(()), dma(()),
     ]
     expert_grad, router_grad, input_grad = pl.pallas_call(
@@ -551,7 +583,7 @@
         ),
         in_specs=[vmem, vmem, vmem],
         out_specs=(hbm, hbm, hbm),
-        scratch_shapes=[dma((3,))],
+        scratch_shapes=[dma((6,))],
         compiler_params=pltpu.CompilerParams(vmem_limit_bytes=2 * 1024 * 1024),
     )(*(pltpu.with_memory_space_constraint(a, pltpu.VMEM) for a in (expert_grad, router_grad, input_grad)))
     return expert_grad.reshape(n * cap, d_cols), router_grad.T, input_grad

time: 70.8 us -> 68.2 us (0.963)
  Pallas kernels: 69.7 us -> 66.7 us
    pallas_call x1, Pallas kernels: 67 us -> 64 us  [body(): pl.pallas_call(kernel, out_shape=(pltpu.VMEM((n, cap, d_cols), BF16), plt...]
where the time goes in v3:
time: 68.2 us; the launch traced here: 67.3 us
  Pallas kernels  66.7 us (98%)
    pallas_call x1, Pallas kernels, body(): pl.pallas_call(kernel, out_shape=(pltpu.VMEM((n, cap, d_cols), BF16), plt...  64 us
    pallas_call x1, Pallas kernels, body(): pl.pallas_call(write_out, out_shape=(jax.ShapeDtypeStruct((n, cap, d_cols...  2.72 us

profile of v3, /device:TPU:0, one launch (start us, length us, event | category | flops | bytes accessed | tf_op | source)
XLA Modules:
  0.0 67.3 jit_solution(10924420182631334659)
XLA Ops:
  0.6 64.0 %shard_map.85 = (bf16[16,192,896]{2,1,0:T(8,128)(2,1)S(1)}, f32[16,896]{1,0:T(8,128)S(1)}, bf16[384,896]{1,0:T(8,128)(2,1)S(1)}) custom-call(bf16[384,896]{1,0:T(8,128)(2,1)} %tok_hbm.1, bf16[384,896]{1,0:T(8,128)(2,1)} %grad_hbm.1, bf16[896,256]{1,0:T(8,128)(2,1)} %weight_hbm.1, bf16[16,192,896]{2,1,0:T(8,128)(2,1)} %bitcast.5, s32[8,384]{1,0:T(8,128)} %bitcast.6, ...), custom_call_target="tpu_custom_call" | custom-call | tf_op jit(solution)/shard_map/pallas_call | solution.py:560
  64.6 2.7 %shard_map.86 = (bf16[16,192,896]{2,1,0:T(8,128)(2,1)}, f32[16,896]{1,0:T(8,128)}, bf16[384,896]{1,0:T(8,128)(2,1)}) custom-call(bf16[16,192,896]{2,1,0:T(8,128)(2,1)S(1)} %get-tuple-element.9.eg_in, f32[16,896]{1,0:T(8,128)S(1)} %get-tuple-element.10.rg_in, bf16[384,896]{1,0:T(8,128)(2,1)S(1)} %get-tuple-element.11.ig_in), custom_call_target="tpu_custom_call" | custom-call | tf_op jit(solution)/shard_map/pallas_call | solution.py:577

commit v4 on v3

--- a/solution.py
+++ b/solution.py
@@ -26,15 +26,17 @@
 LATE_ONES = DIAGONAL + BESIDE
 EARLY, LATE = 8, 8
 ROUNDS = 4
+JOINED = (((0, 1), (2, 1)), ((0, 3), (2, 3)), ((1, 0), (1, 2)), ((3, 0), (3, 2)))
+TERMS = SELF + FAR_ONE + FAR_BOTH + DIAGONAL + BESIDE
 
 
 def kernel(
     tok_hbm, grad_hbm, weight_hbm, eo_hbm, ids_hbm, slots_hbm,
     egv, rg_ref, ig_ref,
     x0, x1, rs0, rs1, rl0, rl1, tok, weight, eo, ids_ref, slots_ref, oh,
-    tb_own, tb_in0, tb_in1, tbf0, tbf1, slot_own, eloc, lsend, win, gsend, gin, dsend, rin, win2,
-    ggv, picked_v, lgt32, lgt, rb, rr,
-    known, in_sem, xs, xr, tbs, tbr, ws, wr, gs, gr, ss, sr, rls, rlr, rts, rtr, w2s, w2r, rps, rpr,
+    tb_own0, tb_own1, tb_in0, tb_in1, tbf0, tbf1, slot_f32, slot_own, eloc, lsend, win, gsend, gin, dsend, rin, win2,
+    ggv, picked_v, lgt32, lgt, rb, rr, rm,
+    known, in_sem, xs, xr, tbs, tbr, ws, wr, gs, gr, ss, sr, rls, rlr, rts, rtr, w2s, w2r, rps, rpr, rms,
 ):
     n = lax.axis_size("expert")
     n_width = lax.axis_size("width")
@@ -45,7 +47,7 @@
     t_half = t_rows // 2
     half = cap // 2
     xs_of, rs_of, rl_of = (x0, x1), (rs0, rs1), (rl0, rl1)
-    tb_in, tbf = (tb_in0, tb_in1), (tbf0, tbf1)
+    tb_own, tb_in, tbf = (tb_own0, tb_own1), (tb_in0, tb_in1), (tbf0, tbf1)
     c0 = x0.shape[2]
     cols = ((0, c0), (c0, x1.shape[2]))
     core = lax.rem(mw, 2)
@@ -104,8 +106,6 @@
         pl.semaphore_wait(known.at[k], len(BESIDE) + 3)
         if k + 1 < ROUNDS:
             greet(known.at[k + 1])
-
-    greet(barrier)
 
     loads = [
         pltpu.make_async_copy(src, dst, in_sem.at[i])
@@ -119,9 +119,11 @@
             (eo_hbm, eo),
         ))
     ]
-    for load in loads:
-        load.start()
-
+    loads[0].start()
+    loads[1].start()
+    greet(barrier)
+    loads[2].start()
+    loads[3].start()
     pl.semaphore_wait(barrier, len(BESIDE) + 3)
 
     def first_copy(g, k):
@@ -137,13 +139,17 @@
         return to(xs_of[g].at[step % SIDE, rows], xs_of[g].at[2, rows], xs.at[g], xr.at[g, 3], e=ring1(g, step))
 
     def table_copy(g, j):
-        return to(tb_own, tb_in[g].at[j], tbs.at[g], tbr.at[g, j // 2 * (3 - j)], e=ring1(g, j))
+        return to(
+            tb_own[g].at[mod(p1[g] + j)], tb_in[g].at[j], tbs.at[g], tbr.at[g, j // 2 * (3 - j)], e=ring1(g, j)
+        )
 
     for g in range(2):
         loads[g].wait()
         first_copy(g, 0).start()
         first_copy(g, 1).start()
     greet(known.at[0])
+    loads[4].start()
+    loads[5].start()
     loads[2].wait()
     loads[3].wait()
     row16 = lax.broadcasted_iota(I32, (n, t_rows), 0)
@@ -158,9 +164,15 @@
     slot_own[...] = slot_tbl
     eloc[...] = eloc_tbl
     slot_f = slot_tbl.astype(F32)
-    tbf0[0] = slot_f
-    tbf1[0] = slot_f
-    tb_own[...] = slot_f.astype(BF16)
+    slot_f32[...] = slot_f
+    for a1 in range(SIDE):
+        by_y = slot_f[a1 * SIDE : (a1 + 1) * SIDE, :]
+        by_z = jnp.concatenate([slot_f[a2 * SIDE + a1 : a2 * SIDE + a1 + 1, :] for a2 in range(SIDE)], axis=0)
+        for g in range(2):
+            rows = by_z + flip[g].astype(F32) * (by_y - by_z)
+            tb_own[g][a1] = rows.astype(BF16)
+    for g in range(2):
+        tbf[g][0] = tb_own[g][p1[g]].astype(F32)
     dsend[...] = jnp.zeros_like(dsend)
 
     for g in range(2):
@@ -169,6 +181,7 @@
     for g in range(2):
         first_copy(g, 2).start()
         first_copy(g, 3).start()
+    loads[6].start()
 
     loads[4].wait()
     loads[5].wait()
@@ -185,7 +198,7 @@
     slot_iota = lax.broadcasted_iota(I32, (ROW, t_rows), 0).astype(F32)
 
     def own_table(d, carry):
-        row = tbf0[0, pl.ds(d, 1), :]
+        row = slot_f32[pl.ds(d, 1), :]
         oh[d] = jnp.where(row == slot_iota, 1.0, 0.0).astype(BF16)
         return carry
 
@@ -210,7 +223,7 @@
             j = j0 + step * i
             picks = []
             for m in range(SIDE):
-                row = tbf[g][j, pl.ds(ring2(g, m), 1), :]
+                row = tbf[g][j, pl.ds(mod(p2[g] + m), 1), :]
                 picks.append(jnp.where(row == cap_iota, 1.0, 0.0).astype(BF16))
             rows = jnp.dot(jnp.concatenate(picks, axis=0), xs_of[g][j], preferred_element_type=F32).astype(BF16)
             rs_of[g][place(g, p1[g] - j, p2[g])] = rows[:cap]
@@ -273,6 +286,21 @@
     send_far(0)
     send_near(0, 0, half)
 
+    def take_tables(js):
+        for g in range(2):
+            await_recv(tb_in[g].at[pl.ds(0, len(js))], tbr.at[g, len(js) % 2])
+            for j in js:
+                tbf[g][j] = tb_in[g][j].astype(F32)
+
+    take_tables((1, 3))
+    for g in range(2):
+        await_recv(xs_of[g].at[0], xr.at[g, 2])
+    for g in range(2):
+        select(g, 1, 2, 2)
+    send_far(1)
+    send_far(3)
+    pass_on(0)
+
     await_recv(win.at[pl.ds(0, n_width - 1)], wr)
     total_logits = win[0]
     for w in range(1, win.shape[0]):
@@ -281,13 +309,11 @@
     picked_v[...] = picked
     gates = (ROUTE_SCALE * picked / jnp.sum(picked, axis=0, keepdims=True)).astype(BF16).astype(F32)
 
-    def gate_row(d, acc):
-        only = jnp.where(row16 == d, gates, 0.0).astype(BF16)
-        return acc + lax.dot_general(only, oh[d], NT, preferred_element_type=F32)
-
-    gate_slots = lax.fori_loop(0, n, gate_row, jnp.zeros((n, ROW), F32))
-    for d in range(n):
-        gsend[d] = gate_slots[d : d + 1, :]
+    gates = gates.astype(BF16)
+    for first in range(0, n, 4):
+        found = [lax.dot_general(gates, oh[d], NT, preferred_element_type=F32) for d in range(first, first + 4)]
+        for i, rows in enumerate(found):
+            gsend[first + i] = rows[first + i : first + i + 1, :]
     gin[me] = gsend[me]
 
     take_round(2)
@@ -302,20 +328,6 @@
 
     lax.fori_loop(1, n, send_gates, 0)
 
-    def take_tables(js):
-        for g in range(2):
-            await_recv(tb_in[g].at[pl.ds(0, len(js))], tbr.at[g, len(js) % 2])
-            for j in js:
-                tbf[g][j] = tb_in[g][j].astype(F32)
-
-    take_tables((1, 3))
-    for g in range(2):
-        await_recv(xs_of[g].at[0], xr.at[g, 2])
-    for g in range(2):
-        select(g, 1, 2, 2)
-    send_far(1)
-    send_far(3)
-    pass_on(0)
     take_tables((2,))
     for g in range(2):
         await_recv(xs_of[g].at[0], xr.at[g, 3])
@@ -463,16 +475,26 @@
 
     part = jnp.dot(lgt[...], tok[...], preferred_element_type=F32)
     rb[...] = part.astype(BF16).reshape(rb.shape)
-
+    rr[0] = rb[me]
+
+    def send_terms(offsets):
+        for dy, dz in offsets:
+            d = target(dy, dz)
+            to(rb.at[d], rr.at[TERMS.index((dy, dz))], rps, rpr, e=d).start()
+
+    for k, (step, owner) in enumerate(JOINED):
+        to(rb.at[target(*owner)], rm.at[k], rps, rms, e=target(*step)).start()
+    send_terms(FAR_BOTH + DIAGONAL + BESIDE)
     logit_grads = lgt32[...].T.astype(BF16)
-    for dy, dz in FAR_BOTH + FAR_NEAR + FAR_ONE + DIAGONAL + BESIDE:
-        d = target(dy, dz)
-        to(rb.at[d], rr.at[me], rps, rpr, e=d).start()
-    rr[me] = rb[me]
     ig_ref[...] = lax.dot_general(logit_grads, weight[...], NT, preferred_element_type=F32).astype(BF16)
-    await_recv(rb.at[pl.ds(0, n - 1)], rpr)
+    await_recv(rm, rms)
+    for k, owner in ((0, (2, 0)), (2, (0, 2))):
+        d = target(*owner)
+        rb[d] = (rb[d].astype(F32) + rm[k].astype(F32) + rm[k + 1].astype(F32)).astype(BF16)
+    send_terms(FAR_ONE)
+    await_recv(rr.at[pl.ds(0, len(TERMS) - 1)], rpr)
     total = rr[0].astype(F32)
-    for d in range(1, n):
+    for d in range(1, len(TERMS)):
         total = total + rr[d].astype(F32)
     rg_ref[...] = total
 
@@ -490,7 +512,7 @@
 
 
 def write_out(eg_in, rg_in, ig_in, eg_out, rg_out, ig_out, sem):
-    pieces = 4
+    pieces = 1
     step = eg_in.shape[0] // pieces
     pairs = [(eg_in.at[pl.ds(i * step, step)], eg_out.at[pl.ds(i * step, step)]) for i in range(pieces)]
     pairs += [(ig_in, ig_out), (rg_in, rg_out)]
@@ -525,11 +547,13 @@
         pltpu.VMEM((top, t_rows), I32),
         pltpu.VMEM((top, t_rows), I32),
         pltpu.VMEM((n, ROW, t_rows), BF16),
-        pltpu.VMEM((n, t_rows), BF16),
-        pltpu.VMEM((SIDE, n, t_rows), BF16),
-        pltpu.VMEM((SIDE, n, t_rows), BF16),
-        pltpu.VMEM((SIDE, n, t_rows), F32),
-        pltpu.VMEM((SIDE, n, t_rows), F32),
+        pltpu.VMEM((SIDE, SIDE, t_rows), BF16),
+        pltpu.VMEM((SIDE, SIDE, t_rows), BF16),
+        pltpu.VMEM((SIDE, SIDE, t_rows), BF16),
+        pltpu.VMEM((SIDE, SIDE, t_rows), BF16),
+        pltpu.VMEM((SIDE, SIDE, t_rows), F32),
+        pltpu.VMEM((SIDE, SIDE, t_rows), F32),
+        pltpu.VMEM((n, t_rows), F32),
         pltpu.VMEM((n, t_rows), I32),
         pltpu.VMEM((n, t_rows), I32),
         pltpu.VMEM((n, t_rows), F32),
@@ -544,7 +568,8 @@
         pltpu.VMEM((experts, t_rows), F32),
         pltpu.VMEM((experts, t_rows), BF16),
         pltpu.VMEM((n, experts // n, d_cols), BF16),
-        pltpu.VMEM((n, experts // n, d_cols), BF16),
+        pltpu.VMEM((len(TERMS), experts // n, d_cols), BF16),
+        pltpu.VMEM((len(JOINED), experts // n, d_cols), BF16),
         pltpu.SemaphoreType.REGULAR((ROUNDS,)),
         dma((7,)),
         dma((2,)), dma((2, 4)),
@@ -555,7 +580,7 @@
         dma((2,)), dma((2, SIDE)),
         dma((2,)), dma(()),
         dma(()), dma((2,)),
-        dma(()), dma(()),
+        dma(()), dma(()), dma(()),
     ]
     expert_grad, router_grad, input_grad = pl.pallas_call(
         kernel,
@@ -583,7 +608,7 @@
         ),
         in_specs=[vmem, vmem, vmem],
         out_specs=(hbm, hbm, hbm),
-        scratch_shapes=[dma((6,))],
+        scratch_shapes=[dma((3,))],
         compiler_params=pltpu.CompilerParams(vmem_limit_bytes=2 * 1024 * 1024),
     )(*(pltpu.with_memory_space_constraint(a, pltpu.VMEM) for a in (expert_grad, router_grad, input_grad)))
     return expert_grad.reshape(n * cap, d_cols), router_grad.T, input_grad

time: 68.2 us -> 67 us (0.982); the launches traced: 67.3 us -> 66.9 us
  no operation moved by 1% of the time
where the time goes in v4:
time: 67 us; the launch traced here: 66.9 us
  Pallas kernels  66.3 us (99%)
    pallas_call x1, Pallas kernels, body(): pl.pallas_call(kernel, out_shape=(pltpu.VMEM((n, cap, d_cols), BF16), plt...  63.6 us
    pallas_call x1, Pallas kernels, body(): pl.pallas_call(write_out, out_shape=(jax.ShapeDtypeStruct((n, cap, d_cols...  2.69 us

profile of v4, /device:TPU:0, one launch (start us, length us, event | category | flops | bytes accessed | tf_op | source)
XLA Modules:
  0.0 66.9 jit_solution(16450325086351957352)
XLA Ops:
  0.6 63.6 %shard_map.85 = (bf16[16,192,896]{2,1,0:T(8,128)(2,1)S(1)}, f32[16,896]{1,0:T(8,128)S(1)}, bf16[384,896]{1,0:T(8,128)(2,1)S(1)}) custom-call(bf16[384,896]{1,0:T(8,128)(2,1)} %tok_hbm.1, bf16[384,896]{1,0:T(8,128)(2,1)} %grad_hbm.1, bf16[896,256]{1,0:T(8,128)(2,1)} %weight_hbm.1, bf16[16,192,896]{2,1,0:T(8,128)(2,1)} %bitcast.5, s32[8,384]{1,0:T(8,128)} %bitcast.6, ...), custom_call_target="tpu_custom_call" | custom-call | tf_op jit(solution)/shard_map/pallas_call | solution.py:585
  64.2 2.7 %shard_map.86 = (bf16[16,192,896]{2,1,0:T(8,128)(2,1)}, f32[16,896]{1,0:T(8,128)}, bf16[384,896]{1,0:T(8,128)(2,1)}) custom-call(bf16[16,192,896]{2,1,0:T(8,128)(2,1)S(1)} %get-tuple-element.9.eg_in, f32[16,896]{1,0:T(8,128)S(1)} %get-tuple-element.10.rg_in, bf16[384,896]{1,0:T(8,128)(2,1)S(1)} %get-tuple-element.11.ig_in), custom_call_target="tpu_custom_call" | custom-call | tf_op jit(solution)/shard_map/pallas_call | solution.py:602

commit v5 on v4

--- a/solution.py
+++ b/solution.py
@@ -34,9 +34,9 @@
     tok_hbm, grad_hbm, weight_hbm, eo_hbm, ids_hbm, slots_hbm,
     egv, rg_ref, ig_ref,
     x0, x1, rs0, rs1, rl0, rl1, tok, weight, eo, ids_ref, slots_ref, oh,
-    tb_own0, tb_own1, tb_in0, tb_in1, tbf0, tbf1, slot_f32, slot_own, eloc, lsend, win, gsend, gin, dsend, rin, win2,
+    tb_own0, tb_own1, tb_in, tbf0, tbf1, slot_f32, slot_own, eloc, lsend, win, gsend, gin, dsend, rin, win2,
     ggv, picked_v, lgt32, lgt, rb, rr, rm,
-    known, in_sem, xs, xr, tbs, tbr, ws, wr, gs, gr, ss, sr, rls, rlr, rts, rtr, w2s, w2r, rps, rpr, rms,
+    known, in_sem, xs, xr, tbs, tbr, ws, wr, gs, gr, ss, sr, rlr, rts, rtr, w2s, w2r, rps, rpr, rms,
 ):
     n = lax.axis_size("expert")
     n_width = lax.axis_size("width")
@@ -46,8 +46,9 @@
     cap = rs0.shape[1]
     t_half = t_rows // 2
     half = cap // 2
+    cut = half
     xs_of, rs_of, rl_of = (x0, x1), (rs0, rs1), (rl0, rl1)
-    tb_own, tb_in, tbf = (tb_own0, tb_own1), (tb_in0, tb_in1), (tbf0, tbf1)
+    tb_own, tbf = (tb_own0, tb_own1), (tbf0, tbf1)
     c0 = x0.shape[2]
     cols = ((0, c0), (c0, x1.shape[2]))
     core = lax.rem(mw, 2)
@@ -130,17 +131,17 @@
         step, h = ((1, 0), (-1, 1), (1, 1), (-1, 0))[k]
         rows = pl.ds(h * t_half, t_half)
         return to(
-            xs_of[g].at[0, rows], xs_of[g].at[step % SIDE, rows], xs.at[g], xr.at[g, min(k, 2)], e=ring1(g, step)
+            xs_of[g].at[0, rows], xs_of[g].at[step % SIDE, rows], xs, xr.at[2 * g + k if k < 2 else 4], e=ring1(g, step)
         )
 
     def onward_copy(g, k):
         step, h = ((1, 0), (-1, 1))[k]
         rows = pl.ds(h * t_half, t_half)
-        return to(xs_of[g].at[step % SIDE, rows], xs_of[g].at[2, rows], xs.at[g], xr.at[g, 3], e=ring1(g, step))
+        return to(xs_of[g].at[step % SIDE, rows], xs_of[g].at[2, rows], xs, xr.at[5], e=ring1(g, step))
 
     def table_copy(g, j):
         return to(
-            tb_own[g].at[mod(p1[g] + j)], tb_in[g].at[j], tbs.at[g], tbr.at[g, j // 2 * (3 - j)], e=ring1(g, j)
+            tb_own[g].at[mod(p1[g] + j)], tb_in.at[g, j], tbs, tbr.at[j // 2 * (3 - j)], e=ring1(g, j)
         )
 
     for g in range(2):
@@ -238,23 +239,23 @@
 
     def near_copy(g, j, kind, start, rows):
         step = (1, -1)[kind]
-        rows = pl.ds(start, rows)
+        part = pl.ds(start, rows)
         return to(
-            rs_of[g].at[n + j * SIDE + step % SIDE, rows], rs_of[g].at[place(g, p1[g] - j, p2[g]), rows],
-            ss.at[g], sr.at[g, (0, 1, 2, 1)[j]], e=ring2(g, step),
+            rs_of[g].at[n + j * SIDE + step % SIDE, part], rs_of[g].at[place(g, p1[g] - j, p2[g]), part],
+            ss, sr.at[(6 if start == 0 else 0, 1, 2, 1)[j]], e=ring2(g, step),
         )
 
     def relay_copy(g, j, h):
         return to(
             rs_of[g].at[n + j * SIDE + 2, pl.ds(h * half, half)], rl_of[g].at[j, h],
-            ss.at[g], rlr.at[g, j], e=ring2(g, (1, -1)[h]),
+            ss, rlr.at[j], e=ring2(g, (1, -1)[h]),
         )
 
     def final_copy(g, j, h):
         step = (1, -1)[h]
         return to(
             rl_of[g].at[j, h], rs_of[g].at[place(g, p1[g] - j, p2[g] - step), pl.ds(h * half, half)],
-            rls.at[g], sr.at[g, 3 + (0, 1, 2, 1)[j]], e=ring2(g, step),
+            ss, sr.at[3 + (0, 1, 2, 1)[j]], e=ring2(g, step),
         )
 
     def send_far(j):
@@ -263,8 +264,8 @@
             relay_copy(g, j, 1).start()
 
     def pass_on(j):
+        await_recv(eo.at[0], rlr.at[j])
         for g in range(2):
-            await_recv(rl_of[g].at[j], rlr.at[g, j])
             final_copy(g, j, 0).start()
             final_copy(g, j, 1).start()
 
@@ -273,28 +274,26 @@
             near_copy(g, j, 0, start, rows).start()
             near_copy(g, j, 1, start, rows).start()
 
-    def arrived(index, count):
-        for g in range(2):
-            await_recv(rs_of[g].at[pl.ds(0, count)], sr.at[g, index])
+    def arrived(index, count, rows=cap):
+        await_recv(eo.at[pl.ds(0, count), pl.ds(0, rows)], sr.at[index])
 
     for g in range(2):
         select(g, 0, 0, 1)
     for k in range(2):
         for g in range(2):
-            await_recv(xs_of[g].at[0, pl.ds(0, t_half)], xr.at[g, k])
+            await_recv(xs_of[g].at[0, pl.ds(0, t_half)], xr.at[2 * g + k])
             onward_copy(g, k).start()
     send_far(0)
-    send_near(0, 0, half)
+    send_near(0, 0, cut)
 
     def take_tables(js):
+        await_recv(tb_in.at[:, pl.ds(0, len(js))], tbr.at[len(js) % 2])
         for g in range(2):
-            await_recv(tb_in[g].at[pl.ds(0, len(js))], tbr.at[g, len(js) % 2])
             for j in js:
-                tbf[g][j] = tb_in[g][j].astype(F32)
+                tbf[g][j] = tb_in[g, j].astype(F32)
 
     take_tables((1, 3))
-    for g in range(2):
-        await_recv(xs_of[g].at[0], xr.at[g, 2])
+    await_recv(tok, xr.at[4])
     for g in range(2):
         select(g, 1, 2, 2)
     send_far(1)
@@ -329,8 +328,7 @@
     lax.fori_loop(1, n, send_gates, 0)
 
     take_tables((2,))
-    for g in range(2):
-        await_recv(xs_of[g].at[0], xr.at[g, 3])
+    await_recv(tok, xr.at[5])
     for g in range(2):
         select(g, 2, 0, 1)
     send_far(2)
@@ -344,21 +342,21 @@
     ones = jnp.ones((8, 256), BF16)
     eye = lax.broadcasted_iota(I32, (cap, cap), 0) == lax.broadcasted_iota(I32, (cap, cap), 1)
 
-    def gate_grads_of(blocks):
+    def gate_grads_of(blocks, start=0, stop=cap):
         found = []
         for s in blocks:
             acc = None
             for g in range(2):
                 for at in range(0, cols[g][1], 128):
-                    a = rs_of[g][s, :, at : at + 128].astype(F32)
-                    b = eo[s, :, cols[g][0] + at : cols[g][0] + at + 128].astype(F32)
+                    a = rs_of[g][s, start:stop, at : at + 128].astype(F32)
+                    b = eo[s, start:stop, cols[g][0] + at : cols[g][0] + at + 128].astype(F32)
                     acc = a * b if acc is None else acc + a * b
             high = acc.astype(BF16)
             low = (acc - high.astype(F32)).astype(BF16)
             both = jnp.concatenate([high, low], axis=1)
             found.append(lax.dot_general(ones, both, NT, preferred_element_type=F32)[0:1, :])
         for s, dots in zip(blocks, found):
-            dsend[s, :, :cap] = dots
+            dsend[s, :, start:stop] = dots
 
     def expert_grad_of(s):
         scale = jnp.where(eye, gin[s][:, :cap], 0.0).astype(BF16)
@@ -384,14 +382,14 @@
         blocks = [origin(dy, dz) for dy, dz in offsets]
         gate_grads_of(blocks)
         for i, s in enumerate(blocks):
-            to(dsend.at[s], rin.at[row + i], rts.at[0], rtr, e=s).start()
+            to(dsend.at[s], rin.at[row + i], rts, rtr, e=s).start()
 
     def late_copy(s, row, w):
-        return to(dsend.at[s], win2.at[mw, row], rts.at[1], w2r.at[1], e=s, w=w)
-
-    def grads_to_widths(offsets, row):
+        return to(dsend.at[s], win2.at[mw, row], w2s, w2r.at[1], e=s, w=w)
+
+    def grads_to_widths(offsets, row, start=0):
         blocks = [origin(dy, dz) for dy, dz in offsets]
-        gate_grads_of(blocks)
+        gate_grads_of(blocks, start)
 
         def one(w, carry):
             for i, s in enumerate(blocks):
@@ -430,17 +428,19 @@
     arrived(5, 1)
     grads_back(FAR_BOTH, 7)
     send_near(3)
-    send_near(0, half, half)
+    send_near(0, cut, cap - cut)
     take_round(3)
     scaled(4, far_near)
     scaled(1, lambda i: (2, 2))
+    arrived(6, 2, cut)
+    gate_grads_of([origin(dy, dz) for dy, dz in BESIDE], 0, cut)
     await_recv(dsend.at[pl.ds(0, EARLY - 1)], rtr)
     lax.fori_loop(1, n_width, send_width, 0)
     win2[mw, rows] = rin[...]
     arrived(1, 4)
     grads_to_widths(DIAGONAL, EARLY)
-    arrived(0, 2)
-    grads_to_widths(BESIDE, EARLY + len(DIAGONAL))
+    arrived(0, 2, cap - cut)
+    grads_to_widths(BESIDE, EARLY + len(DIAGONAL), cut)
     scaled(4, diagonal)
     scaled(4, beside)
 
@@ -498,16 +498,13 @@
         total = total + rr[d].astype(F32)
     rg_ref[...] = total
 
-    for g in range(2):
-        await_sent(xs_of[g].at[pl.ds(0, SIDE - 1)], xs.at[g])
-        await_sent(tb_in[g].at[pl.ds(0, SIDE - 1)], tbs.at[g])
-        await_sent(rs_of[g].at[pl.ds(0, (SIDE - 1) * SIDE)], ss.at[g])
-        await_sent(rl_of[g], rls.at[g])
+    await_sent(eo.at[pl.ds(0, (SIDE - 1) * t_rows // cap)], xs)
+    await_sent(tb_in.at[:, pl.ds(0, SIDE - 1)], tbs)
+    await_sent(eo, ss)
     await_sent(win.at[pl.ds(0, n_width - 1)], ws)
     await_sent(gin.at[pl.ds(0, n - 1)], gs)
-    await_sent(dsend.at[pl.ds(0, EARLY - 1)], rts.at[0])
-    await_sent(win2.at[pl.ds(0, n_width), pl.ds(0, LATE)], rts.at[1])
-    await_sent(win2.at[pl.ds(0, n_width - 1), pl.ds(0, EARLY)], w2s)
+    await_sent(dsend.at[pl.ds(0, EARLY - 1)], rts)
+    await_sent(win2.at[pl.ds(0, n_width), pl.ds(0, n - 1)], w2s)
     await_sent(rb.at[pl.ds(0, n - 1)], rps)
 
 
@@ -549,8 +546,7 @@
         pltpu.VMEM((n, ROW, t_rows), BF16),
         pltpu.VMEM((SIDE, SIDE, t_rows), BF16),
         pltpu.VMEM((SIDE, SIDE, t_rows), BF16),
-        pltpu.VMEM((SIDE, SIDE, t_rows), BF16),
-        pltpu.VMEM((SIDE, SIDE, t_rows), BF16),
+        pltpu.VMEM((2, SIDE, SIDE, t_rows), BF16),
         pltpu.VMEM((SIDE, SIDE, t_rows), F32),
         pltpu.VMEM((SIDE, SIDE, t_rows), F32),
         pltpu.VMEM((n, t_rows), F32),
@@ -572,13 +568,12 @@
         pltpu.VMEM((len(JOINED), experts // n, d_cols), BF16),
         pltpu.SemaphoreType.REGULAR((ROUNDS,)),
         dma((7,)),
-        dma((2,)), dma((2, 4)),
-        dma((2,)), dma((2, 2)),
+        dma(()), dma((6,)),
+        dma(()), dma((2,)),
         dma(()), dma(()),
         dma(()), dma(()),
-        dma((2,)), dma((2, 6)),
-        dma((2,)), dma((2, SIDE)),
-        dma((2,)), dma(()),
+        dma(()), dma((7,)), dma((SIDE,)),
+        dma(()), dma(()),
         dma(()), dma((2,)),
         dma(()), dma(()), dma(()),
     ]

time: 67 us -> 66.7 us (level)
  no operation moved by 1% of the time
where the time goes in v5:
time: 66.7 us; the launch traced here: 66.6 us
  Pallas kernels  65.9 us (99%)
    pallas_call x1, Pallas kernels, body(): pl.pallas_call(kernel, out_shape=(pltpu.VMEM((n, cap, d_cols), BF16), plt...  63.2 us
    pallas_call x1, Pallas kernels, body(): pl.pallas_call(write_out, out_shape=(jax.ShapeDtypeStruct((n, cap, d_cols...  2.69 us

profile of v5, /device:TPU:0, one launch (start us, length us, event | category | flops | bytes accessed | tf_op | source)
XLA Modules:
  0.0 66.6 jit_solution(15850858869623580786)
XLA Ops:
  0.6 63.2 %shard_map.85 = (bf16[16,192,896]{2,1,0:T(8,128)(2,1)S(1)}, f32[16,896]{1,0:T(8,128)S(1)}, bf16[384,896]{1,0:T(8,128)(2,1)S(1)}) custom-call(bf16[384,896]{1,0:T(8,128)(2,1)} %tok_hbm.1, bf16[384,896]{1,0:T(8,128)(2,1)} %grad_hbm.1, bf16[896,256]{1,0:T(8,128)(2,1)} %weight_hbm.1, bf16[16,192,896]{2,1,0:T(8,128)(2,1)} %bitcast.5, s32[8,384]{1,0:T(8,128)} %bitcast.6, ...), custom_call_target="tpu_custom_call" | custom-call | tf_op jit(solution)/shard_map/pallas_call | solution.py:580
  63.9 2.7 %shard_map.86 = (bf16[16,192,896]{2,1,0:T(8,128)(2,1)}, f32[16,896]{1,0:T(8,128)}, bf16[384,896]{1,0:T(8,128)(2,1)}) custom-call(bf16[16,192,896]{2,1,0:T(8,128)(2,1)S(1)} %get-tuple-element.9.eg_in, f32[16,896]{1,0:T(8,128)S(1)} %get-tuple-element.10.rg_in, bf16[384,896]{1,0:T(8,128)(2,1)S(1)} %get-tuple-element.11.ig_in), custom_call_target="tpu_custom_call" | custom-call | tf_op jit(solution)/shard_map/pallas_call | solution.py:597

commit v6 on v5

--- a/solution.py
+++ b/solution.py
@@ -484,7 +484,7 @@
 
     for k, (step, owner) in enumerate(JOINED):
         to(rb.at[target(*owner)], rm.at[k], rps, rms, e=target(*step)).start()
-    send_terms(FAR_BOTH + DIAGONAL + BESIDE)
+    send_terms(FAR_BOTH + BESIDE + DIAGONAL)
     logit_grads = lgt32[...].T.astype(BF16)
     ig_ref[...] = lax.dot_general(logit_grads, weight[...], NT, preferred_element_type=F32).astype(BF16)
     await_recv(rm, rms)

time: 66.7 us -> 66.7 us (level)
  no operation moved by 1% of the time
where the time goes in v6:
time: 66.7 us; the launch traced here: 66.6 us
  Pallas kernels  65.9 us (99%)
    pallas_call x1, Pallas kernels, body(): pl.pallas_call(kernel, out_shape=(pltpu.VMEM((n, cap, d_cols), BF16), plt...  63.2 us
    pallas_call x1, Pallas kernels, body(): pl.pallas_call(write_out, out_shape=(jax.ShapeDtypeStruct((n, cap, d_cols...  2.69 us

profile of v6, /device:TPU:0, one launch (start us, length us, event | category | flops | bytes accessed | tf_op | source)
XLA Modules:
  0.0 66.6 jit_solution(7050024141581359578)
XLA Ops:
  0.6 63.2 %shard_map.85 = (bf16[16,192,896]{2,1,0:T(8,128)(2,1)S(1)}, f32[16,896]{1,0:T(8,128)S(1)}, bf16[384,896]{1,0:T(8,128)(2,1)S(1)}) custom-call(bf16[384,896]{1,0:T(8,128)(2,1)} %tok_hbm.1, bf16[384,896]{1,0:T(8,128)(2,1)} %grad_hbm.1, bf16[896,256]{1,0:T(8,128)(2,1)} %weight_hbm.1, bf16[16,192,896]{2,1,0:T(8,128)(2,1)} %bitcast.5, s32[8,384]{1,0:T(8,128)} %bitcast.6, ...), custom_call_target="tpu_custom_call" | custom-call | tf_op jit(solution)/shard_map/pallas_call | solution.py:580
  63.9 2.7 %shard_map.86 = (bf16[16,192,896]{2,1,0:T(8,128)(2,1)}, f32[16,896]{1,0:T(8,128)}, bf16[384,896]{1,0:T(8,128)(2,1)}) custom-call(bf16[16,192,896]{2,1,0:T(8,128)(2,1)S(1)} %get-tuple-element.9.eg_in, f32[16,896]{1,0:T(8,128)S(1)} %get-tuple-element.10.rg_in, bf16[384,896]{1,0:T(8,128)(2,1)S(1)} %get-tuple-element.11.ig_in), custom_call_target="tpu_custom_call" | custom-call | tf_op jit(solution)/shard_map/pallas_call | solution.py:597

commit v7 on v5

--- a/solution.py
+++ b/solution.py
@@ -120,9 +120,9 @@
             (eo_hbm, eo),
         ))
     ]
+    greet(barrier)
     loads[0].start()
     loads[1].start()
-    greet(barrier)
     loads[2].start()
     loads[3].start()
     pl.semaphore_wait(barrier, len(BESIDE) + 3)
@@ -475,7 +475,6 @@
 
     part = jnp.dot(lgt[...], tok[...], preferred_element_type=F32)
     rb[...] = part.astype(BF16).reshape(rb.shape)
-    rr[0] = rb[me]
 
     def send_terms(offsets):
         for dy, dz in offsets:
@@ -485,6 +484,7 @@
     for k, (step, owner) in enumerate(JOINED):
         to(rb.at[target(*owner)], rm.at[k], rps, rms, e=target(*step)).start()
     send_terms(FAR_BOTH + DIAGONAL + BESIDE)
+    rr[0] = rb[me]
     logit_grads = lgt32[...].T.astype(BF16)
     ig_ref[...] = lax.dot_general(logit_grads, weight[...], NT, preferred_element_type=F32).astype(BF16)
     await_recv(rm, rms)

time: 66.7 us -> 66.7 us (level)
  no operation moved by 1% of the time
where the time goes in v7:
time: 66.7 us; the launch traced here: 66.6 us
  Pallas kernels  66 us (99%)
    pallas_call x1, Pallas kernels, body(): pl.pallas_call(kernel, out_shape=(pltpu.VMEM((n, cap, d_cols), BF16), plt...  63.3 us
    pallas_call x1, Pallas kernels, body(): pl.pallas_call(write_out, out_shape=(jax.ShapeDtypeStruct((n, cap, d_cols...  2.69 us

profile of v7, /device:TPU:0, one launch (start us, length us, event | category | flops | bytes accessed | tf_op | source)
XLA Modules:
  0.0 66.6 jit_solution(14750189921131149024)
XLA Ops:
  0.6 63.3 %shard_map.85 = (bf16[16,192,896]{2,1,0:T(8,128)(2,1)S(1)}, f32[16,896]{1,0:T(8,128)S(1)}, bf16[384,896]{1,0:T(8,128)(2,1)S(1)}) custom-call(bf16[384,896]{1,0:T(8,128)(2,1)} %tok_hbm.1, bf16[384,896]{1,0:T(8,128)(2,1)} %grad_hbm.1, bf16[896,256]{1,0:T(8,128)(2,1)} %weight_hbm.1, bf16[16,192,896]{2,1,0:T(8,128)(2,1)} %bitcast.5, s32[8,384]{1,0:T(8,128)} %bitcast.6, ...), custom_call_target="tpu_custom_call" | custom-call | tf_op jit(solution)/shard_map/pallas_call | solution.py:580
  63.9 2.7 %shard_map.86 = (bf16[16,192,896]{2,1,0:T(8,128)(2,1)}, f32[16,896]{1,0:T(8,128)}, bf16[384,896]{1,0:T(8,128)(2,1)}) custom-call(bf16[16,192,896]{2,1,0:T(8,128)(2,1)S(1)} %get-tuple-element.9.eg_in, f32[16,896]{1,0:T(8,128)S(1)} %get-tuple-element.10.rg_in, bf16[384,896]{1,0:T(8,128)(2,1)S(1)} %get-tuple-element.11.ig_in), custom_call_target="tpu_custom_call" | custom-call | tf_op jit(solution)/shard_map/pallas_call | solution.py:597

commit v8 on v7

--- a/solution.py
+++ b/solution.py
@@ -242,7 +242,7 @@
         part = pl.ds(start, rows)
         return to(
             rs_of[g].at[n + j * SIDE + step % SIDE, part], rs_of[g].at[place(g, p1[g] - j, p2[g]), part],
-            ss, sr.at[(6 if start == 0 else 0, 1, 2, 1)[j]], e=ring2(g, step),
+            ss, sr.at[(6 if start == 0 else 0, 7, 2, 1)[j]], e=ring2(g, step),
         )
 
     def relay_copy(g, j, h):
@@ -391,12 +391,9 @@
         blocks = [origin(dy, dz) for dy, dz in offsets]
         gate_grads_of(blocks, start)
 
-        def one(w, carry):
+        for o in sorted(range(n_width), key=lambda o: -min(o, n_width - o)):
             for i, s in enumerate(blocks):
-                late_copy(s, row + i, w).start()
-            return carry
-
-        lax.fori_loop(0, n_width, one, 0)
+                late_copy(s, row + i, lax.rem(mw + o, n_width)).start()
 
     def scaled(count, offset):
         def one(i, carry):
@@ -434,11 +431,13 @@
     scaled(1, lambda i: (2, 2))
     arrived(6, 2, cut)
     gate_grads_of([origin(dy, dz) for dy, dz in BESIDE], 0, cut)
+    arrived(7, 2)
+    grads_to_widths(DIAGONAL[:1], EARLY)
     await_recv(dsend.at[pl.ds(0, EARLY - 1)], rtr)
     lax.fori_loop(1, n_width, send_width, 0)
     win2[mw, rows] = rin[...]
-    arrived(1, 4)
-    grads_to_widths(DIAGONAL, EARLY)
+    arrived(1, 2)
+    grads_to_widths(DIAGONAL[1:], EARLY + 1)
     arrived(0, 2, cap - cut)
     grads_to_widths(BESIDE, EARLY + len(DIAGONAL), cut)
     scaled(4, diagonal)
@@ -572,7 +571,7 @@
         dma(()), dma((2,)),
         dma(()), dma(()),
         dma(()), dma(()),
-        dma(()), dma((7,)), dma((SIDE,)),
+        dma(()), dma((8,)), dma((SIDE,)),
         dma(()), dma(()),
         dma(()), dma((2,)),
         dma(()), dma(()), dma(()),

time: 66.7 us -> 66.9 us (level)
  no operation moved by 1% of the time
where the time goes in v8:
time: 66.9 us; the launch traced here: 66.7 us
  Pallas kernels  66.1 us (99%)
    pallas_call x1, Pallas kernels, body(): pl.pallas_call(kernel, out_shape=(pltpu.VMEM((n, cap, d_cols), BF16), plt...  63.4 us
    pallas_call x1, Pallas kernels, body(): pl.pallas_call(write_out, out_shape=(jax.ShapeDtypeStruct((n, cap, d_cols...  2.69 us

profile of v8, /device:TPU:0, one launch (start us, length us, event | category | flops | bytes accessed | tf_op | source)
XLA Modules:
  0.0 66.7 jit_solution(9723166469078545535)
XLA Ops:
  0.6 63.4 %shard_map.85 = (bf16[16,192,896]{2,1,0:T(8,128)(2,1)S(1)}, f32[16,896]{1,0:T(8,128)S(1)}, bf16[384,896]{1,0:T(8,128)(2,1)S(1)}) custom-call(bf16[384,896]{1,0:T(8,128)(2,1)} %tok_hbm.1, bf16[384,896]{1,0:T(8,128)(2,1)} %grad_hbm.1, bf16[896,256]{1,0:T(8,128)(2,1)} %weight_hbm.1, bf16[16,192,896]{2,1,0:T(8,128)(2,1)} %bitcast.5, s32[8,384]{1,0:T(8,128)} %bitcast.6, ...), custom_call_target="tpu_custom_call" | custom-call | tf_op jit(solution)/shard_map/pallas_call | solution.py:579
  64.1 2.7 %shard_map.86 = (bf16[16,192,896]{2,1,0:T(8,128)(2,1)}, f32[16,896]{1,0:T(8,128)}, bf16[384,896]{1,0:T(8,128)(2,1)}) custom-call(bf16[16,192,896]{2,1,0:T(8,128)(2,1)S(1)} %get-tuple-element.9.eg_in, f32[16,896]{1,0:T(8,128)S(1)} %get-tuple-element.10.rg_in, bf16[384,896]{1,0:T(8,128)(2,1)S(1)} %get-tuple-element.11.ig_in), custom_call_target="tpu_custom_call" | custom-call | tf_op jit(solution)/shard_map/pallas_call | solution.py:596
